TPU v7x, 128 devices: a whole 4x4x4 slice. The times are simulated.
128 devices in a mesh: task: 8 (over x_hi, y), tp: 16 (over z, x_lo, core).
Axes of the slice: x: 4 (x_hi: 2, x_lo: 2; x = x_hi * 2 + x_lo), y: 4, z: 4, core: 2. Of those that a mesh axis runs over, the one named last changes fastest.
Arguments:
- observations: bfloat16 [256, 16, 4096], P('task', None, 'tp'), may hold values from -6 to 6
- gain: float32 [4096], P('tp'), may hold values from 0.5 to 1.5
- w_in: bfloat16 [4096, 4096], P(None, 'tp'), may hold values from -0.09375 to 0.09375
- w_mix: bfloat16 [4096, 4096], P('tp'), may hold values from -0.09375 to 0.09375
- w_out: bfloat16 [4096, 4096], P(None, 'tp'), may hold values from -0.09375 to 0.09375
- w_head: bfloat16 [4096, 75], P('tp'), may hold values from -0.09375 to 0.09375
- head_bias: float32 [75], replicated, may hold values from -4 to 4
- pop_mean: float32 [57], replicated, may hold values from -8 to 8
- pop_scale: float32 [57], replicated, may hold values from 0.5 to 4
- task_indices: int32 [256], P('task'), may hold values from 0 to 56
- actions: int32 [256, 15], P('task'), may hold values from 0 to 17
- rewards: float32 [256, 15], P('task'), may hold values from -18 to 27
- episode_ends: int32 [256, 15], P('task'), may hold values 0 or 1
- behaviour_log_prob: float32 [256, 15], P('task'), may hold values from -4.5 to -1.5
Outputs:
- grad_w_in: float32 [4096, 4096], P(None, 'tp')
- grad_w_mix: float32 [4096, 4096], P('tp')
- grad_w_out: float32 [4096, 4096], P(None, 'tp')
- grad_gain: float32 [4096], P('tp')
- grad_head: float32 [4096, 75], P('tp')
- grad_head_bias: float32 [75], replicated
- new_head: bfloat16 [4096, 75], P('tp')
- new_bias: float32 [75], replicated
- updated_return_mean: float32 [57], replicated
- updated_return_scale: float32 [57], replicated
All inputs are finite; a program needn't handle non-finite values. No bound on the sum of `episode_ends` on one device may be relied on, other than what follows from the above.
Results may differ from a plain program's by a relative error of at most 0.03.
Values may be sent and summed in bfloat16 or wider, within the bound.
A program may use at most 128 MiB of HBM per device.

v0:
```python
import jax
import jax.numpy as jnp
from jax import lax
from jax.sharding import PartitionSpec as P

ACTIONS = 18
TASKS = 57


DISCOUNT = 0.99
BASELINE_COST = 0.5
ENTROPY_COST = 0.01
POPART_PRIOR = 64.0
NORM_EPS = 1e-06


def sent_to_all(value, axis):
    copies = jnp.broadcast_to(value, (lax.axis_size(axis), *value.shape))
    return lax.all_to_all(copies, axis, split_axis=0, concat_axis=0, tiled=True)


def of_everyone(value, axis):
    everything = sent_to_all(value, axis)
    return jnp.sum(everything, axis=0)


def packed_total(arrays, axis):
    line, at, gathered = (jnp.concatenate([a.reshape(-1) for a in arrays]), 0, [])
    subtotal = of_everyone(line, axis)
    for a in arrays:
        gathered.append(subtotal[at : at + a.size].reshape(a.shape))
        at += a.size
    return tuple(gathered)


def cut_along(value, dim, devices):
    before, after = (value.shape[:dim], value.shape[dim + 1 :])
    return jnp.moveaxis(value.reshape(*before, devices, -1, *after), dim, 0)


def sum_at_owner(value, axis, dim):
    parts = cut_along(value, dim, lax.axis_size(axis))
    arrived = lax.all_to_all(parts, axis, split_axis=0, concat_axis=0, tiled=True)
    return arrived.astype(jnp.float32).sum(axis=0)


def joined_along(parts, dim):
    dims = list(parts.shape[1:])
    dims[dim] *= parts.shape[0]
    return jnp.moveaxis(parts, 0, dim).reshape(dims)


def gathered_copies(value, axis, dim):
    parts = sent_to_all(value, axis)
    return joined_along(parts, dim)


def summed_on_arrival(value, axis, dim):
    parts = cut_along(value, dim, lax.axis_size(axis))
    arrived = lax.all_to_all(parts, axis, split_axis=0, concat_axis=0, tiled=True)
    return arrived.sum(axis=0)


def silu_slope(before):
    sigmoid = jax.nn.sigmoid(before)
    return sigmoid * (1.0 + before * (1.0 - sigmoid))


def discounted_sums(values, factors):

    def advance(running, column):
        latest = column[0] + column[1] * running
        return (latest, latest)

    opening = jnp.zeros((values.shape[0],), jnp.float32)
    ending, stacked = lax.scan(advance, opening, (values.T, factors.T), reverse=True)
    return stacked.T


def task_onehot(task_indices):
    return (task_indices[:, None] == jnp.arange(TASKS, dtype=jnp.int32)[None, :]).astype(
        jnp.float32
    )


def popart_partials(task_indices, rewards, discount_factors):
    returns = discounted_sums(rewards, discount_factors)
    task_table = task_onehot(task_indices)
    counts = jnp.sum(task_table, axis=0) * rewards.shape[1]
    totals = jnp.dot(task_table.T, jnp.sum(returns, axis=1))
    squares = jnp.dot(task_table.T, jnp.sum(returns * returns, axis=1))
    return (counts, totals, squares)


def popart_update(counts, totals, squares, pop_mean, pop_scale):
    mixing = counts / (counts + POPART_PRIOR)
    safe_counts = jnp.maximum(counts, 1.0)
    batch_mean = totals / safe_counts
    batch_square = squares / safe_counts
    updated_return_mean = (1.0 - mixing) * pop_mean + mixing * batch_mean
    mean_gap = batch_mean - pop_mean
    variance = (
        (1.0 - mixing) * pop_scale * pop_scale
        + mixing * (batch_square - batch_mean * batch_mean)
        + mixing * (1.0 - mixing) * mean_gap * mean_gap
    )
    return (updated_return_mean, jnp.sqrt(variance))


def rescale_head(w_head, head_bias, pop_mean, pop_scale, updated_return_mean, updated_return_scale):
    scale_ratio = pop_scale / updated_return_scale
    column_scale = jnp.concatenate([jnp.ones((ACTIONS,), jnp.float32), scale_ratio])
    new_head = (w_head.astype(jnp.float32) * column_scale[None, :]).astype(jnp.bfloat16)
    value_bias = (
        pop_scale * head_bias[ACTIONS:] + pop_mean - updated_return_mean
    ) / updated_return_scale
    new_bias = jnp.concatenate([head_bias[:ACTIONS], value_bias])
    return (new_head, new_bias)


def importance_trace_loss(
    head_value_estimates,
    task_indices,
    actions,
    rewards,
    discount_factors,
    behaviour_log_prob,
    updated_return_mean,
    updated_return_scale,
    loss_weighting,
):
    task_table = task_onehot(task_indices)
    env_mean = jnp.dot(task_table, updated_return_mean)[:, None]
    env_scale = jnp.dot(task_table, updated_return_scale)[:, None]
    logits = head_value_estimates[:, :-1, :ACTIONS]
    norm_values = jnp.sum(head_value_estimates[:, :, ACTIONS:] * task_table[:, None, :], axis=2)
    values = lax.stop_gradient(norm_values * env_scale + env_mean)
    log_total = jnp.log(jnp.sum(jnp.exp(logits), axis=2))
    chosen = actions[:, :, None] == jnp.arange(ACTIONS, dtype=jnp.int32)[None, None, :]
    log_policy = jnp.sum(jnp.where(chosen, logits, 0.0), axis=2) - log_total
    clipped = jnp.minimum(jnp.exp(lax.stop_gradient(log_policy) - behaviour_log_prob), 1.0)
    deltas = clipped * (rewards + discount_factors * values[:, 1:] - values[:, :-1])
    targets = values[:, :-1] + discounted_sums(deltas, discount_factors * clipped)
    following = jnp.concatenate([targets[:, 1:], values[:, -1:]], axis=1)
    advantage = lax.stop_gradient(
        clipped
        * ((rewards + discount_factors * following - env_mean) / env_scale - norm_values[:, :-1])
    )
    normed_targets = lax.stop_gradient((targets - env_mean) / env_scale)
    policy = jnp.exp(logits - log_total[:, :, None])
    entropy = -jnp.sum(policy * (logits - log_total[:, :, None]), axis=2)
    per_frame = (
        -advantage * log_policy
        + 0.5 * BASELINE_COST * (normed_targets - norm_values[:, :-1]) ** 2
        - ENTROPY_COST * entropy
    )
    return loss_weighting * jnp.sum(per_frame)


def on_device(
    observations,
    gain,
    w_in,
    w_mix,
    w_out,
    w_head,
    head_bias,
    pop_mean,
    pop_scale,
    task_indices,
    actions,
    rewards,
    episode_ends,
    behaviour_log_prob,
):
    env_count, frames, part_width = observations.shape
    groups = lax.axis_size("tp")
    full_width = part_width * groups
    row_count = env_count * frames
    local_rows = row_count // groups
    own_tokens = observations.reshape(row_count, part_width)
    discount_factors = DISCOUNT * (1.0 - episode_ends.astype(jnp.float32))
    counts, totals, squares = popart_partials(task_indices, rewards, discount_factors)
    counts, totals, squares = packed_total((counts, totals, squares), "task")
    updated_return_mean, updated_return_scale = popart_update(
        counts, totals, squares, pop_mean, pop_scale
    )
    new_head, new_bias = rescale_head(
        w_head, head_bias, pop_mean, pop_scale, updated_return_mean, updated_return_scale
    )
    loss_weighting = float(env_count * lax.axis_size("task")) ** (-0.5)
    tokens, gain_all = (
        lax.all_gather(own_tokens, "tp", axis=1, tiled=True),
        lax.all_gather(gain.astype(jnp.bfloat16), "tp", axis=0, tiled=True).astype(gain.dtype),
    )
    row_offset = lax.axis_index("tp") * local_rows
    token_rows = lax.dynamic_slice_in_dim(tokens, row_offset, local_rows, 0)
    pre_in = jnp.dot(tokens, w_in, preferred_element_type=jnp.float32)
    hidden_in = jax.nn.silu(pre_in).astype(jnp.bfloat16)
    hidden_rows = hidden_in
    mix_sum = lax.psum_scatter(
        jnp.dot(hidden_rows, w_mix, preferred_element_type=jnp.float32).astype(jnp.bfloat16),
        "tp",
        scatter_dimension=0,
        tiled=True,
    ).astype(jnp.float32)
    residual = token_rows.astype(jnp.float32) + mix_sum
    inverse = lax.rsqrt(jnp.mean(residual * residual, axis=1, keepdims=True) + NORM_EPS)
    normed = (residual * inverse * gain_all[None, :]).astype(jnp.bfloat16)
    normed_all = lax.all_gather(normed, "tp", axis=0, tiled=True)
    pre_out = jnp.dot(normed_all, w_out, preferred_element_type=jnp.float32)
    hidden_out = jax.nn.silu(pre_out).astype(jnp.bfloat16)
    head_terms = jnp.dot(hidden_out, new_head, preferred_element_type=jnp.float32)
    env_share = env_count // groups
    env_offset = lax.axis_index("tp") * env_share

    def select_envs(source):
        return lax.dynamic_slice_in_dim(source, env_offset, env_share, 0)

    head_value_estimates = (
        sum_at_owner(head_terms.astype(jnp.bfloat16), "tp", 0) + new_bias[None, :]
    )
    head_value_estimates = head_value_estimates.reshape(env_share, frames, -1)

    def share_loss(network_outputs):
        return importance_trace_loss(
            network_outputs,
            select_envs(task_indices),
            select_envs(actions),
            select_envs(rewards),
            select_envs(discount_factors),
            select_envs(behaviour_log_prob),
            updated_return_mean,
            updated_return_scale,
            loss_weighting,
        )

    loss_value, pullback = jax.vjp(share_loss, head_value_estimates)
    (d_heads,) = pullback(jnp.ones((), jnp.float32))
    d_local = d_heads.reshape(env_share * frames, -1).astype(jnp.bfloat16)
    d_rounded = gathered_copies(d_local, "tp", 0)
    grad_head = jnp.dot(hidden_out.T, d_rounded, preferred_element_type=jnp.float32)
    grad_bias = jnp.sum(d_rounded.astype(jnp.float32), axis=0)
    d_hidden_out = jnp.dot(d_rounded, new_head.T, preferred_element_type=jnp.float32)
    d_pre_out = (d_hidden_out * silu_slope(pre_out)).astype(jnp.bfloat16)
    grad_out = jnp.dot(normed_all.T, d_pre_out, preferred_element_type=jnp.float32)
    d_normed = lax.psum_scatter(
        jnp.dot(d_pre_out, w_out.T, preferred_element_type=jnp.float32).astype(jnp.bfloat16),
        "tp",
        scatter_dimension=0,
        tiled=True,
    ).astype(jnp.float32)
    scaled = d_normed * gain_all[None, :]
    inner_sum = jnp.sum(scaled * residual, axis=1, keepdims=True)
    d_residual = (inverse * scaled - residual * inverse**3 * inner_sum / full_width).astype(
        jnp.bfloat16
    )
    grad_gain = summed_on_arrival(jnp.sum(d_normed * residual * inverse, axis=0), "tp", 0)
    arrived = lax.all_gather(d_residual, "tp", axis=0, tiled=True)
    hidden_rows = hidden_in
    grad_part = jnp.dot(hidden_rows.T, arrived, preferred_element_type=jnp.float32)
    d_hidden = jnp.dot(arrived, w_mix.T, preferred_element_type=jnp.float32)
    grad_mix = grad_part
    d_pre_in = (d_hidden * silu_slope(pre_in)).astype(jnp.bfloat16)
    grad_in = jnp.dot(tokens.T, d_pre_in, preferred_element_type=jnp.float32)
    grad_in, grad_mix, grad_out, grad_gain, grad_head, grad_bias = (
        lax.psum(grad_in.astype(jnp.bfloat16), "task").astype(jnp.float32),
        lax.psum(grad_mix.astype(jnp.bfloat16), "task").astype(jnp.float32),
        lax.psum(grad_out.astype(jnp.bfloat16), "task").astype(jnp.float32),
        lax.psum(grad_gain.astype(jnp.bfloat16), "task").astype(jnp.float32),
        lax.psum(grad_head.astype(jnp.bfloat16), "task").astype(jnp.float32),
        lax.psum(grad_bias.astype(jnp.bfloat16), "task").astype(jnp.float32),
    )
    return (
        grad_in,
        grad_mix,
        grad_out,
        grad_gain,
        grad_head,
        grad_bias,
        new_head,
        new_bias,
        updated_return_mean,
        updated_return_scale,
    )


def solution(mesh):
    in_specs = (
        P("task", None, "tp"),
        P("tp"),
        P(None, "tp"),
        P("tp", None),
        P(None, "tp"),
        P("tp", None),
        P(),
        P(),
        P(),
        P("task"),
        P("task", None),
        P("task", None),
        P("task", None),
        P("task", None),
    )
    out_specs = (
        P(None, "tp"),
        P("tp", None),
        P(None, "tp"),
        P("tp"),
        P("tp", None),
        P(),
        P("tp", None),
        P(),
        P(),
        P(),
    )
    return jax.shard_map(
        on_device, mesh=mesh, in_specs=in_specs, out_specs=out_specs, check_vma=False
    )
```

profile of v0, /device:TPU:1, one launch (start us, length us, event | category | flops | bytes accessed | tf_op | source)
XLA Modules:
  0.0 498.5 jit_solution(18199204609391938755)
XLA Ops:
  8.0 50.4 %all-gather.5.cloned.1.call-done = bf16[512,4096]{1,0:T(8,128)(2,1)} async-done(((bf16[512,256]{1,0:T(8,128)(2,1)}), bf16[512,4096]{1,0:T(8,128)(2,1)}) %all-gather.5.cloned.1.call-update) | async-done | bytes 4194320 | tf_op jit(solution)/shard_map/all_gather | solution.py:193
  58.4 4.1 fusion.46
  62.5 3.3 convolution_convert_fusion.1
  66.0 18.6 %all-gather = bf16[16,1,256]{2,1,0:T(2,128)(2,1)S(1)} all-gather(bf16[1,1,256]{2,1,0:T(2,128)(2,1)S(1)} %reshape.98), channel_id=1, replica_groups=mesh['task'=8,'tp'=16] {'tp'}, dimensions={0}, use_global_device_ids=true | all-gather | bytes 8704 | tf_op jit(solution)/shard_map/all_gather | solution.py:194
  84.6 49.5 %reduce-scatter.3.cloned.1.call-done = bf16[32,4096]{1,0:T(8,128)(2,1)} async-done(((bf16[512,4096]{1,0:T(8,128)(2,1)}), bf16[32,4096]{1,0:T(8,128)(2,1)}) %reduce-scatter.3.cloned.1.call-update) | async-done | bytes 262160 | tf_op jit(solution)/shard_map/reduce_scatter | solution.py:201
  140.1 6.2 %all-to-all-start = ((f32[8,1,171]{2,1,0:T(1,128)}), f32[8,1,171]{2,1,0:T(1,128)S(1)}, u32[]{:S(2)}, u32[]{:S(2)}) async-start(f32[8,1,171]{2,1,0:T(1,128)} %broadcast_in_dim.72), calls=%async_computation.1 | async-start | bytes 16384 | tf_op jit(solution)/shard_map/all_to_all | solution.py:19
  146.9 6.0 %all-to-all-done = f32[8,1,171]{2,1,0:T(1,128)S(1)} async-done(((f32[8,1,171]{2,1,0:T(1,128)}), f32[8,1,171]{2,1,0:T(1,128)S(1)}, u32[]{:S(2)}, u32[]{:S(2)}) %all-to-all-start) | async-done | bytes 5504 | tf_op jit(solution)/shard_map/all_to_all | solution.py:19
  153.6 23.3 %all-gather.7.cloned.1.call-done = bf16[512,4096]{1,0:T(8,128)(2,1)} async-done(((bf16[32,4096]{1,0:T(8,128)(2,1)}), bf16[512,4096]{1,0:T(8,128)(2,1)}) %all-gather.7.cloned.1.call-update) | async-done | bytes 4194320 | tf_op jit(solution)/shard_map/all_gather | solution.py:210
  176.8 4.9 multiply_convert_fusion
  182.8 4.2 all-to-all-start.1
  187.0 6.0 %all-to-all-done.1 = bf16[16,32,75]{2,1,0:T(8,128)(2,1)S(1)} async-done(((bf16[16,32,75]{2,1,0:T(8,128)(2,1)}), bf16[16,32,75]{2,1,0:T(8,128)(2,1)S(1)}, u32[]{:S(2)}, u32[]{:S(2)}) %all-to-all-start.1) | async-done | bytes 76832 | tf_op jit(solution)/shard_map/all_to_all | solution.py:43
  195.7 9.4 %all_to_all.25 = bf16[16,32,75]{2,1,0:T(8,128)(2,1)S(1)} all-to-all(bf16[16,32,75]{2,1,0:T(8,128)(2,1)S(1)} %broadcast_in_dim.79), channel_id=1, replica_groups=mesh['task'=8,'tp'=16] {'tp'}, dimensions={0} | all-to-all | bytes 153600 | tf_op jit(solution)/shard_map/all_to_all | solution.py:19
  206.4 3.3 convolution_convert_fusion
  209.8 67.0 %reduce-scatter.5.cloned.1.call-done = bf16[32,4096]{1,0:T(8,128)(2,1)} async-done(((bf16[512,4096]{1,0:T(8,128)(2,1)}), bf16[32,4096]{1,0:T(8,128)(2,1)}) %reduce-scatter.5.cloned.1.call-update) | async-done | bytes 262160 | tf_op jit(solution)/shard_map/reduce_scatter | solution.py:247
  280.9 4.8 convolution_convert_fusion.2
  285.7 33.9 %all-gather.9.cloned.1.call-done = bf16[512,4096]{1,0:T(8,128)(2,1)} async-done(((bf16[32,4096]{1,0:T(8,128)(2,1)}), bf16[512,4096]{1,0:T(8,128)(2,1)}) %all-gather.9.cloned.1.call-update) | async-done | bytes 4194320 | tf_op jit(solution)/shard_map/all_gather | solution.py:259
  319.6 9.4 %fusion.4 = bf16[4096,256]{0,1:T(8,128)(2,1)} fusion(bf16[512,4096]{1,0:T(8,128)(2,1)} %all-gather.5.cloned.1.call-done, bf16[512,4096]{1,0:T(8,128)(2,1)} %all-gather.9.cloned.1.call-done, bf16[256,4096]{1,0:T(8,128)(2,1)S(1)} %copy-done, f32[512,256]{1,0:T(8,128)S(1)} %fusion.46), kind=kOutput, calls=%fused_computation.11 | convolution fusion | flops 2149711872 | bytes 13107200 | tf_op jit(solution)/shard_map/dot_general | solution.py:265
  329.0 4.8 convolution_convert_fusion.3
  333.8 4.4 all-to-all-start.3
  338.5 5.5 %all-to-all-done.3 = f32[16,1,256]{2,1,0:T(1,128)S(1)} async-done(((f32[16,1,256]{2,1,0:T(1,128)}), f32[16,1,256]{2,1,0:T(1,128)S(1)}, u32[]{:S(2)}, u32[]{:S(2)}) %all-to-all-start.3) | async-done | bytes 16416 | tf_op jit(solution)/shard_map/all_to_all | solution.py:60
  344.0 38.7 %all-reduce.4 = (bf16[256]{0:T(256)(128)(2,1)S(1)}, bf16[256,75]{0,1:T(8,128)(2,1)S(1)}, bf16[75]{0:T(256)(128)(2,1)S(1)}) all-reduce(bf16[256]{0:T(256)(128)(2,1)S(1)} %reduce_sum.162, bf16[256,75]{0,1:T(8,128)(2,1)S(1)} %convolution_convert_fusion.6, bf16[75]{0:T(256)(128)(2,1)S(1)} %reduce_sum.163), channel_id=1, replica_groups=mesh['task'=8,'tp'=16] {'task'}, use_global_device_ids=true, to_apply=%region_23.24 | all-reduce | flops 19531 | bytes 78124 | tf_op jit(solution)/shard_map/psum | solution.py:270
  384.4 96.4 %all-reduce.8.cloned.1.call-done = (bf16[4096,256]{0,1:T(8,128)(2,1)}, bf16[256,4096]{1,0:T(8,128)(2,1)}, bf16[4096,256]{1,0:T(8,128)(2,1)}) async-done(((bf16[4096,256]{0,1:T(8,128)(2,1)}, bf16[256,4096]{1,0:T(8,128)(2,1)}, bf16[4096,256]{1,0:T(8,128)(2,1)}), (bf16[4096,256]{0,1:T(8,128)(2,1)}, bf16[256,4096]{1,0:T(8,128)(2,1)}, bf16[4096,256]{1,0:T(8,128)(2,1)})) %all-reduce.8.cloned.1.call-update) | async-done | bytes 6291472 | tf_op jit(solution)/shard_map/psum | solution.py:267
  480.8 4.3 copy.105
  485.1 4.2 convert_element_type.134
  (180 shorter events, 23.4 us)
Async XLA Ops:
  7.2 55.3 %copy-start = (bf16[256,4096]{1,0:T(8,128)(2,1)S(1)}, bf16[256,4096]{1,0:T(8,128)(2,1)}, u32[]{:S(2)}) copy-start(bf16[256,4096]{1,0:T(8,128)(2,1)} %param.21) | copy-start | bytes 6291460
  7.2 51.2 %all-gather.5.cloned.1.call-start = ((), (), s32[]{:S(2)}) async-start(), calls=%async_computation.6 | async-start | bytes 4456448 | tf_op jit(solution)/shard_map/all_gather | solution.py:193
  7.9 126.2 %reduce-scatter.3.cloned.1.call-start = ((), (), s32[]{:S(2)}) async-start(), calls=%async_computation.7 | async-start | bytes 4456448 | tf_op jit(solution)/shard_map/reduce_scatter | solution.py:201
  65.8 71.9 %copy-start.7 = (s32[32,15]{0,1:T(8,128)S(1)}, s32[32,15]{0,1:T(8,128)}, u32[]{:S(2)}) copy-start(s32[32,15]{0,1:T(8,128)} %param.30) | copy-start | bytes 5764
  65.8 72.1 %copy-start.6 = (f32[32,15]{0,1:T(8,128)S(1)}, f32[32,15]{0,1:T(8,128)}, u32[]{:S(2)}) copy-start(f32[32,15]{0,1:T(8,128)} %param.29) | copy-start | bytes 5764
  65.8 73.3 %copy-start.18 = (s32[32]{0:T(128)S(1)}, s32[32]{0:T(128)}, u32[]{:S(2)}) copy-start(s32[32]{0:T(128)} %param.27) | copy-start | bytes 388
  65.8 80.6 %copy-start.9 = (f32[32,15]{0,1:T(8,128)S(1)}, f32[32,15]{0,1:T(8,128)}, u32[]{:S(2)}) copy-start(f32[32,15]{0,1:T(8,128)} %param.31) | copy-start | bytes 5764
  65.8 80.7 %copy-start.8 = (s32[32,15]{0,1:T(8,128)S(1)}, s32[32,15]{0,1:T(8,128)}, u32[]{:S(2)}) copy-start(s32[32,15]{0,1:T(8,128)} %param.28) | copy-start | bytes 5764
  65.8 87.1 %copy-start.12 = (f32[57]{0:T(128)S(1)}, f32[57]{0:T(128)}, u32[]{:S(2)}) copy-start(f32[57]{0:T(128)} %param.25) | copy-start | bytes 688
  65.8 87.1 %copy-start.13 = (f32[57]{0:T(128)S(1)}, f32[57]{0:T(128)}, u32[]{:S(2)}) copy-start(f32[57]{0:T(128)} %param.26) | copy-start | bytes 688
  65.8 87.0 %copy-start.14 = (f32[75]{0:T(128)S(1)}, f32[75]{0:T(128)}, u32[]{:S(2)}) copy-start(f32[75]{0:T(128)} %param.24) | copy-start | bytes 904
  65.9 87.6 %copy-start.5 = (bf16[256,75]{0,1:T(8,128)(2,1)S(1)}, bf16[256,75]{0,1:T(8,128)(2,1)}, u32[]{:S(2)}) copy-start(bf16[256,75]{0,1:T(8,128)(2,1)} %param.23) | copy-start | bytes 115204
  65.9 111.0 %all-gather.7.cloned.1.call-start = ((), (), s32[]{:S(2)}) async-start(), calls=%async_computation.8 | async-start | bytes 4456448 | tf_op jit(solution)/shard_map/all_gather | solution.py:210
  140.1 12.7 %all-to-all-start = ((f32[8,1,171]{2,1,0:T(1,128)}), f32[8,1,171]{2,1,0:T(1,128)S(1)}, u32[]{:S(2)}, u32[]{:S(2)}) async-start(f32[8,1,171]{2,1,0:T(1,128)} %broadcast_in_dim.72), calls=%async_computation.1 | async-start | bytes 16384 | tf_op jit(solution)/shard_map/all_to_all | solution.py:19
  153.0 28.8 %copy-start.15 = (f32[57]{0:T(128)}, f32[57]{0:T(128)S(1)}, u32[]{:S(2)}) copy-start(f32[57]{0:T(128)S(1)} %get-tuple-element.394) | copy-start | bytes 688
  153.0 28.8 %copy-start.16 = (f32[57]{0:T(128)}, f32[57]{0:T(128)S(1)}, u32[]{:S(2)}) copy-start(f32[57]{0:T(128)S(1)} %get-tuple-element.395) | copy-start | bytes 688
  153.6 51.5 %copy-start.4 = (bf16[256,75]{0,1:T(8,128)(2,1)}, bf16[256,75]{0,1:T(8,128)(2,1)S(1)}, u32[]{:S(2)}) copy-start(bf16[256,75]{0,1:T(8,128)(2,1)S(1)} %multiply_convert_fusion.3) | copy-start | bytes 115204
  182.8 10.3 %all-to-all-start.1 = ((bf16[16,32,75]{2,1,0:T(8,128)(2,1)}), bf16[16,32,75]{2,1,0:T(8,128)(2,1)S(1)}, u32[]{:S(2)}, u32[]{:S(2)}) async-start(bf16[16,32,75]{2,1,0:T(8,128)(2,1)} %bitcast.8), calls=%async_computation.2 | async-start | bytes 262144 | tf_op jit(solution)/shard_map/all_to_all | solution.py:43
  186.9 89.9 %reduce-scatter.5.cloned.1.call-start = ((), (), s32[]{:S(2)}) async-start(), calls=%async_computation.9 | async-start | bytes 4456448 | tf_op jit(solution)/shard_map/reduce_scatter | solution.py:247
  195.2 11.2 %copy-start.3 = (bf16[4096,256]{1,0:T(8,128)(2,1)S(1)}, bf16[4096,256]{1,0:T(8,128)(2,1)}, u32[]{:S(2)}) copy-start(bf16[4096,256]{1,0:T(8,128)(2,1)} %param.22) | copy-start | bytes 6291460
  209.7 67.1 %copy-start.1 = (bf16[32,4096]{1,0:T(8,128)(2,1)S(1)}, bf16[32,4096]{1,0:T(8,128)(2,1)}, u32[]{:S(2)}) copy-start(bf16[32,4096]{1,0:T(8,128)(2,1)} %reduce-scatter.3.cloned.1.call-done) | copy-start | bytes 786436
  209.7 109.8 %all-gather.9.cloned.1.call-start = ((), (), s32[]{:S(2)}) async-start(), calls=%async_computation.10 | async-start | bytes 4456448 | tf_op jit(solution)/shard_map/all_gather | solution.py:259
  280.6 200.2 %all-reduce.8.cloned.1.call-start = ((), (), s32[]{:S(2)}) async-start(), calls=%async_computation.11 | async-start | bytes 12582912 | tf_op jit(solution)/shard_map/psum | solution.py:267
  333.8 10.1 %all-to-all-start.3 = ((f32[16,1,256]{2,1,0:T(1,128)}), f32[16,1,256]{2,1,0:T(1,128)S(1)}, u32[]{:S(2)}, u32[]{:S(2)}) async-start(f32[16,1,256]{2,1,0:T(1,128)} %bitcast.20), calls=%async_computation.5 | async-start | bytes 32768 | tf_op jit(solution)/shard_map/all_to_all | solution.py:60
  (4 other events, 15.6 us)
Sparse Core Ops, SparseCore 0:
  9.6 48.6 all-gather.4
  66.0 68.0 reduce-scatter.2
  137.8 38.9 all-gather.6
  209.9 66.9 reduce-scatter.4
  280.8 38.7 all-gather.8
  333.9 146.8 all-reduce.7
where the time goes:
time: 499 us
  waiting for transfers between devices  339 us (68%)
  blocking collectives  66.7 us (13%)
  matrix products  37 us (7%)
  other arithmetic  18 us (4%)
  starting transfers between devices  15.1 us (3%)
  between operations  14.4 us (3%)
  local copies, waits for them, and re-layouts  8.14 us (2%)
    psum x1, waiting for transfers between devices, on_device(): lax.psum(grad_in.astype(jnp.bfloat16), 'task').astype(jnp.float32)  96.4 us
    reduce_scatter x1, waiting for transfers between devices, on_device(): lax.psum_scatter(jnp.dot(d_pre_out, w_out.T, preferred_element_type=jnp.f...  67 us
    all_gather x1, waiting for transfers between devices, on_device(): lax.all_gather(own_tokens, 'tp', axis=1, tiled=True)  50.4 us
    reduce_scatter x1, waiting for transfers between devices, on_device(): lax.psum_scatter(jnp.dot(hidden_rows, w_mix, preferred_element_type=jnp.f...  49.5 us
    psum x1, blocking collectives, on_device(): lax.psum(grad_gain.astype(jnp.bfloat16), 'task').astype(jnp.float32)  38.7 us
    all_gather x1, waiting for transfers between devices, on_device(): arrived = lax.all_gather(d_residual, 'tp', axis=0, tiled=True)  33.9 us
    all_gather x1, waiting for transfers between devices, on_device(): normed_all = lax.all_gather(normed, 'tp', axis=0, tiled=True)  23.3 us
    all_gather x1, blocking collectives, on_device(): lax.all_gather(gain.astype(jnp.bfloat16), 'tp', axis=0, tiled=True)  18.6 us
  transfers between devices with their start and end apart: 9, of which 9 were waited for; matrix products, arithmetic and copies ran while one was open for 2% of the time, Pallas kernels for 0%

commit v1 on v0

--- a/solution.py
+++ b/solution.py
@@ -1,6 +1,8 @@
 import jax
 import jax.numpy as jnp
 from jax import lax
+from jax.experimental import pallas as pl
+from jax.experimental.pallas import tpu as pltpu
 from jax.sharding import PartitionSpec as P
 
 ACTIONS = 18
@@ -12,6 +14,779 @@
 ENTROPY_COST = 0.01
 POPART_PRIOR = 64.0
 NORM_EPS = 1e-06
+
+
+MESH = pl.DeviceIdType.MESH
+F32 = jnp.float32
+BF16 = jnp.bfloat16
+HALVES = (0, 1)
+
+
+def plus(a, b, n):
+    return lax.rem(a + b, n)
+
+
+class Place:
+    def __init__(self):
+        self.me = lax.axis_index("tp")
+        self.z = self.me // 4
+        self.x = lax.rem(self.me // 2, 2)
+        self.c = lax.rem(self.me, 2)
+        self.across = self.at(0, 1)
+        self.up = self.at(1, 0)
+        self.down = self.at(3, 0)
+        self.partner = self.at(0, 0, 1)
+
+    def at(self, dz, dx, dc=0):
+        return (plus(self.z, dz, 4) * 2 + plus(self.x, dx, 2)) * 2 + plus(self.c, dc, 2)
+
+    def greet(self):
+        barrier = pltpu.get_barrier_semaphore()
+        peers = (self.across, self.up, self.down, self.partner)
+        for peer in peers:
+            pl.semaphore_signal(barrier, inc=1, device_id={"tp": peer}, device_id_type=MESH)
+        pl.semaphore_wait(barrier, len(peers))
+
+
+def greet_all(task):
+    barrier = pltpu.get_barrier_semaphore()
+    me = lax.axis_index("tp")
+    for hop in range(1, 16):
+        pl.semaphore_signal(
+            barrier, inc=1, device_id={"tp": plus(me, hop, 16)}, device_id_type=MESH
+        )
+    for peer in (task.up, task.down, task.across):
+        pl.semaphore_signal(barrier, inc=1, device_id={"task": peer}, device_id_type=MESH)
+    pl.semaphore_wait(barrier, 18)
+
+
+class Wires:
+    def __init__(self, send_sems, recv_sems):
+        self.send_sems = send_sems
+        self.recv_sems = recv_sems
+        self.sent = []
+        self.slots = 0
+
+    def claim(self, count):
+        first = self.slots
+        self.slots += count
+        return first
+
+    def send(self, src, dst, slot, peer, axis="tp"):
+        copy = pltpu.make_async_remote_copy(
+            src_ref=src,
+            dst_ref=dst,
+            send_sem=self.send_sems.at[len(self.sent)],
+            recv_sem=self.recv_sems.at[slot],
+            device_id={axis: peer},
+            device_id_type=MESH,
+        )
+        copy.start()
+        self.sent.append(copy)
+
+    def arrived(self, dst, slot, axis="tp"):
+        pltpu.make_async_remote_copy(
+            src_ref=dst,
+            dst_ref=dst,
+            send_sem=self.send_sems.at[0],
+            recv_sem=self.recv_sems.at[slot],
+            device_id={axis: lax.axis_index(axis)},
+            device_id_type=MESH,
+        ).wait_recv()
+
+    def drain(self):
+        for copy in self.sent:
+            copy.wait_send()
+
+
+class Gather:
+    ACROSS, FROM_DOWN, FROM_UP, DOWN_ACROSS, UP_ACROSS, FAR, FAR_ACROSS, OWN = range(8)
+
+    def __init__(self, place, wires, view):
+        self.place = place
+        self.wires = wires
+        self.view = view
+        self.first = wires.claim(30)
+        p = place
+        self.block = {
+            self.ACROSS: p.at(0, 1),
+            self.FROM_DOWN: p.at(3, 0),
+            self.FROM_UP: p.at(1, 0),
+            self.DOWN_ACROSS: p.at(3, 1),
+            self.UP_ACROSS: p.at(1, 1),
+            self.FAR: p.at(2, 0),
+            self.FAR_ACROSS: p.at(2, 1),
+            self.OWN: p.me,
+        }
+        self.twin = {k: plus(b, 0, 16) + 1 - 2 * p.c for k, b in self.block.items()}
+
+    def slot(self, kind, half):
+        return self.first + kind * 2 + half
+
+    def twin_slot(self, kind, half):
+        return self.first + 14 + kind * 2 + half
+
+    def pass_on(self, kind, half, peer, kind_there):
+        v = self.view(self.block[kind], half)
+        self.wires.send(v, v, self.slot(kind_there, half), peer)
+
+    def to_twin(self, kind, half):
+        v = self.view(self.block[kind], half)
+        self.wires.send(v, v, self.twin_slot(kind, half), self.place.partner)
+
+    def wait(self, kind, half):
+        self.wires.arrived(self.view(self.block[kind], half), self.slot(kind, half))
+
+    def wait_twin(self, *kinds):
+        for kind in kinds:
+            for half in HALVES:
+                self.wires.arrived(
+                    self.view(self.twin[kind], half), self.twin_slot(kind, half)
+                )
+
+    def open(self):
+        p = self.place
+        for half in HALVES:
+            self.pass_on(self.OWN, half, p.up, self.FROM_DOWN)
+            self.pass_on(self.OWN, half, p.down, self.FROM_UP)
+            self.pass_on(self.OWN, half, p.across, self.ACROSS)
+            self.to_twin(self.OWN, half)
+
+    def middle(self):
+        p = self.place
+        self.wait(self.FROM_DOWN, 0)
+        self.pass_on(self.FROM_DOWN, 0, p.up, self.FAR)
+        self.to_twin(self.FROM_DOWN, 0)
+        self.wait(self.FROM_UP, 0)
+        self.to_twin(self.FROM_UP, 0)
+        self.wait(self.ACROSS, 0)
+        self.pass_on(self.ACROSS, 0, p.down, self.UP_ACROSS)
+        self.wait(self.FROM_UP, 1)
+        self.pass_on(self.FROM_UP, 1, p.down, self.FAR)
+        self.pass_on(self.ACROSS, 0, p.up, self.DOWN_ACROSS)
+        self.to_twin(self.ACROSS, 0)
+        self.to_twin(self.FROM_UP, 1)
+        self.wait(self.FROM_DOWN, 1)
+        self.to_twin(self.FROM_DOWN, 1)
+        self.wait(self.ACROSS, 1)
+        self.pass_on(self.ACROSS, 1, p.up, self.DOWN_ACROSS)
+        self.pass_on(self.ACROSS, 1, p.down, self.UP_ACROSS)
+        self.to_twin(self.ACROSS, 1)
+        for half in HALVES:
+            self.wait(self.FAR, half)
+            self.pass_on(self.FAR, half, p.across, self.FAR_ACROSS)
+            self.to_twin(self.FAR, half)
+
+    def late(self):
+        for half in HALVES:
+            for kind in (self.DOWN_ACROSS, self.UP_ACROSS):
+                self.wait(kind, half)
+                self.to_twin(kind, half)
+
+    def last(self):
+        for half in HALVES:
+            self.wait(self.FAR_ACROSS, half)
+            self.to_twin(self.FAR_ACROSS, half)
+
+
+def half_cols(half):
+    return pl.ds(half * 2048, 2048)
+
+
+class Scatter:
+    G, D, E, F, A, B, C = range(7)
+    ORDER = ((2, 1), (1, 1), (3, 1), (1, 0), (3, 0), (2, 0), (0, 1), (0, 0))
+
+    def __init__(self, place, wires, partial, twin_part, landing):
+        self.place = place
+        self.wires = wires
+        self.partial = partial
+        self.twin_part = twin_part
+        self.landing = landing
+        self.first = wires.claim(30)
+
+    def rows(self, where, dc=0):
+        return pl.ds(pl.multiple_of(self.place.at(*where, dc) * 32, 32), 32)
+
+    def mine(self, where, half):
+        return self.partial.at[self.rows(where), half_cols(half)]
+
+    def twins(self, where, half):
+        return self.twin_part.at[self.ORDER.index(where), :, half_cols(half)]
+
+    def land(self, kind, half):
+        return self.landing.at[kind, :, half_cols(half)]
+
+    def total(self, where, half, kinds=(), waited=()):
+        slot = self.first + 14 + self.ORDER.index(where) * 2 + half
+        if (where, half) not in self.seen:
+            self.wires.arrived(self.twins(where, half), slot)
+            self.seen.add((where, half))
+        for kind in kinds:
+            self.wires.arrived(self.land(kind, half), self.first + kind * 2 + half)
+        value = self.mine(where, half)[...].astype(F32) + self.twins(where, half)[...].astype(F32)
+        for kind in kinds:
+            value = value + self.land(kind, half)[...].astype(F32)
+        return value
+
+    def forward(self, where, half, kinds, peer, kind_there):
+        self.mine(where, half)[...] = self.total(where, half, kinds).astype(BF16)
+        self.wires.send(
+            self.mine(where, half),
+            self.land(kind_there, half),
+            self.first + kind_there * 2 + half,
+            peer,
+        )
+
+    def open(self, produce):
+        self.seen = set()
+        p = self.place
+        for half in HALVES:
+            produce(half)
+            for where in self.ORDER:
+                self.wires.send(
+                    self.partial.at[self.rows(where, 1), half_cols(half)],
+                    self.twins(where, half),
+                    self.first + 14 + self.ORDER.index(where) * 2 + half,
+                    p.partner,
+                )
+            self.forward((2, 1), half, (), p.across, self.G)
+            self.forward((1, 1), half, (), p.up, self.D)
+            self.forward((3, 1), half, (), p.down, self.E)
+        self.forward((1, 0), 1, (), p.up, self.B)
+        self.forward((3, 0), 0, (), p.down, self.C)
+
+    def finish_far(self):
+        p = self.place
+        self.forward((2, 0), 0, (self.G,), p.up, self.F)
+        self.forward((2, 0), 1, (self.G,), p.down, self.F)
+
+    def finish_across(self):
+        for half in HALVES:
+            self.forward((0, 1), half, (self.D, self.E), self.place.across, self.A)
+
+    def finish_near(self):
+        p = self.place
+        self.forward((1, 0), 0, (self.F,), p.up, self.B)
+        self.forward((3, 0), 1, (self.F,), p.down, self.C)
+
+    def finish(self, store):
+        for half in HALVES:
+            store(half, self.total((0, 0), half, (self.A, self.B, self.C)))
+
+
+def sigmoid(v):
+    return 1.0 / (1.0 + jnp.exp(-v))
+
+
+def dot(a, b, contract=((1,), (0,))):
+    return lax.dot_general(a, b, (contract, ((), ())), preferred_element_type=F32)
+
+
+def load(src, dst, sems, at):
+    copy = pltpu.make_async_copy(src, dst, sems.at[at])
+    copy.start()
+    return copy
+
+
+def wide_product(left, right, partial, half, transposed):
+    def tile(n, carry):
+        at = pl.multiple_of(half * 2048 + n * 256, 256)
+        if transposed:
+            value = dot(left[...], right[pl.ds(at, 256), :], ((1,), (1,)))
+        else:
+            value = dot(left[...], right[:, pl.ds(at, 256)])
+        partial[:, pl.ds(at, 256)] = value.astype(BF16)
+        return carry
+
+    lax.fori_loop(0, 8, tile, 0)
+
+
+def row_view(ref):
+    return lambda block, half: ref.at[
+        pl.ds(pl.multiple_of(block * 32, 32), 32), half_cols(half)
+    ]
+
+
+def forward_kernel(
+    own_tokens, gain, w_in, w_mix,
+    tokens_out, pre_in, hidden_in, residual, gain_all, normed_out,
+    tokens, w_in_v, w_mix_v, partial, twin_part, landing, normed,
+    send_sems, recv_sems, local_sems,
+):
+    place = Place()
+    wires = Wires(send_sems, recv_sems)
+    me = place.me
+    own_cols = pl.ds(pl.multiple_of(me * 256, 256), 256)
+    first = load(own_tokens, tokens.at[pl.ds(0, 512), own_cols], local_sems, 0)
+    g = gain[...]
+    hi = g.astype(BF16).astype(F32)
+    mid = (g - hi).astype(BF16).astype(F32)
+    low = g - hi - mid
+    row = lax.broadcasted_iota(jnp.int32, (16, 256), 0)
+    rows = jnp.where(row == 0, hi, jnp.where(row == 1, mid, jnp.where(row == 2, low, 0.0)))
+    tokens[pl.ds(512, 16), own_cols] = rows.astype(BF16)
+    place.greet()
+    first.wait()
+
+    def token_view(block, half):
+        rows = pl.ds(0, 256) if half == 0 else pl.ds(256, 272)
+        return tokens.at[rows, pl.ds(pl.multiple_of(block * 256, 256), 256)]
+
+    gather = Gather(place, wires, token_view)
+    gather.open()
+    get_in = load(w_in, w_in_v, local_sems, 1)
+    get_mix = load(w_mix, w_mix_v, local_sems, 2)
+    gather.middle()
+
+    def slab(dz, opening=False):
+        at = pl.multiple_of(plus(place.z, dz, 4) * 1024, 1024)
+
+        def tile(m, carry):
+            r = pl.ds(pl.multiple_of(m * 128, 128), 128)
+            value = dot(tokens[r, pl.ds(at, 1024)], w_in_v[pl.ds(at, 1024), :])
+            pre_in[r, :] = value if opening else pre_in[r, :] + value
+            return carry
+
+        lax.fori_loop(0, 4, tile, 0)
+
+    get_in.wait()
+    gather.wait_twin(gather.OWN, gather.ACROSS)
+    slab(0, True)
+    gather.late()
+    gather.wait_twin(gather.FROM_UP, gather.UP_ACROSS)
+    slab(1)
+    gather.last()
+    gather.wait_twin(gather.FROM_DOWN, gather.DOWN_ACROSS)
+    slab(3)
+    gather.wait_twin(gather.FAR, gather.FAR_ACROSS)
+    slab(2)
+    keep = load(tokens.at[pl.ds(0, 512), :], tokens_out, local_sems, 3)
+
+    def activate(m, carry):
+        r = pl.ds(pl.multiple_of(m * 128, 128), 128)
+        v = pre_in[r, :]
+        hidden_in[r, :] = (v * sigmoid(v)).astype(BF16)
+        return carry
+
+    lax.fori_loop(0, 4, activate, 0)
+    g3 = tokens[pl.ds(512, 16), :].astype(F32)
+    gain_all[...] = g3[0:1, :] + g3[1:2, :] + g3[2:3, :]
+    get_mix.wait()
+    scatter = Scatter(place, wires, partial, twin_part, landing)
+    scatter.open(lambda half: wide_product(hidden_in, w_mix_v, partial, half, False))
+    own_rows = pl.ds(pl.multiple_of(me * 32, 32), 32)
+
+    def store(half, value):
+        residual[:, half_cols(half)] = (
+            value + tokens[own_rows, half_cols(half)].astype(F32)
+        )
+
+    scatter.finish_far()
+    scatter.finish_across()
+    scatter.finish_near()
+    scatter.finish(store)
+    for m in range(2):
+        v = residual[pl.ds(m * 16, 16), :]
+        inverse = lax.rsqrt(jnp.mean(v * v, axis=1, keepdims=True) + NORM_EPS)
+        normed[pl.ds(pl.multiple_of(me * 32 + m * 16, 16), 16), :] = (
+            v * inverse * gain_all[...]
+        ).astype(BF16)
+    spread = Gather(place, wires, row_view(normed))
+    spread.open()
+    spread.middle()
+    spread.late()
+    spread.last()
+    spread.wait_twin(*range(8))
+    out = load(normed, normed_out, local_sems, 4)
+    keep.wait()
+    out.wait()
+    wires.drain()
+
+
+class TaskPlace:
+    def __init__(self):
+        task = lax.axis_index("task")
+        self.xh = task // 4
+        self.y = lax.rem(task, 4)
+        self.up = self.xh * 4 + plus(self.y, 1, 4)
+        self.down = self.xh * 4 + plus(self.y, 3, 4)
+        self.across = (1 - self.xh) * 4 + self.y
+
+
+class TaskSum:
+    F, B, C = range(3)
+    OWN, FROM_DOWN, FROM_UP, DOWN_ACROSS, UP_ACROSS, FAR, FAR_ACROSS = range(7)
+
+    def __init__(self, place, wires, view, whole, land, land_x, result):
+        self.place = place
+        self.wires = wires
+        self.view = view
+        self.whole = whole
+        self.land = land
+        self.land_x = land_x
+        self.result = result
+        self.first = wires.claim(14)
+
+    def slab(self, ref, dy, part):
+        return self.view(ref, plus(self.place.y, dy, 4) * 2 + part)
+
+    def post(self, src, dst, slot, peer):
+        self.wires.send(src, dst, self.first + slot, peer, "task")
+
+    def wait(self, dst, slot):
+        self.wires.arrived(dst, self.first + slot, "task")
+
+    def far(self):
+        p = self.place
+        self.post(self.slab(self.whole, 2, 0), self.land.at[self.F, 0], 0, p.up)
+        self.post(self.slab(self.whole, 2, 1), self.land.at[self.F, 1], 1, p.down)
+
+    def near(self):
+        p = self.place
+        self.post(self.slab(self.whole, 1, 1), self.land.at[self.B, 1], 3, p.up)
+        self.post(self.slab(self.whole, 3, 0), self.land.at[self.C, 0], 4, p.down)
+
+    def relay(self):
+        p = self.place
+        for dy, part, kind, slot, peer in ((1, 0, self.B, 2, p.up), (3, 1, self.C, 5, p.down)):
+            self.wait(self.land.at[self.F, part], part)
+            own = self.slab(self.whole, dy, part)
+            total = own[...].astype(F32) + self.land[self.F, part].astype(F32)
+            own[...] = total.astype(BF16)
+            self.post(own, self.land.at[kind, part], slot, peer)
+
+    def local(self, part):
+        return (
+            self.slab(self.whole, 0, part)[...].astype(F32)
+            + self.land[self.B, part].astype(F32)
+            + self.land[self.C, part].astype(F32)
+        )
+
+    def fold(self):
+        for kind, part, slot in ((self.B, 1, 3), (self.C, 0, 4), (self.B, 0, 2), (self.C, 1, 5)):
+            self.wait(self.land.at[kind, part], slot)
+        other = 1 - self.place.xh
+        away = self.slab(self.whole, 0, other)
+        away[...] = self.local(other).astype(BF16)
+        self.post(away, self.land_x, 6, self.place.across)
+
+    def pass_on(self, kind, peer, kind_there):
+        v = self.held(kind)
+        self.post(v, v, 6 + kind_there, peer)
+
+    def held(self, kind):
+        dy, across = {
+            self.OWN: (0, 0),
+            self.FROM_DOWN: (3, 0),
+            self.FROM_UP: (1, 0),
+            self.DOWN_ACROSS: (3, 1),
+            self.UP_ACROSS: (1, 1),
+            self.FAR: (2, 0),
+            self.FAR_ACROSS: (2, 1),
+        }[kind]
+        xh = self.place.xh
+        return self.slab(self.result, dy, 1 - xh if across else xh)
+
+    def across_held(self):
+        return self.slab(self.result, 0, 1 - self.place.xh)
+
+    def finish(self):
+        p = self.place
+        self.wait(self.land_x, 6)
+        own = self.held(self.OWN)
+        own[...] = (self.local(p.xh) + self.land_x[...].astype(F32)).astype(BF16)
+        self.post(own, own, 13, p.across)
+        self.pass_on(self.OWN, p.up, self.FROM_DOWN)
+        self.pass_on(self.OWN, p.down, self.FROM_UP)
+
+    def get(self, kind):
+        self.wait(self.held(kind), 6 + kind)
+
+    def spread(self):
+        p = self.place
+        self.get(self.FROM_DOWN)
+        self.pass_on(self.FROM_DOWN, p.up, self.FAR)
+        self.get(self.FROM_UP)
+        v = self.across_held()
+        self.wait(v, 13)
+        self.post(v, v, 6 + self.DOWN_ACROSS, p.up)
+        self.post(v, v, 6 + self.UP_ACROSS, p.down)
+
+    def spread_far(self):
+        self.get(self.UP_ACROSS)
+        self.pass_on(self.UP_ACROSS, self.place.down, self.FAR_ACROSS)
+        self.get(self.DOWN_ACROSS)
+
+    def end(self):
+        self.get(self.FAR)
+        self.get(self.FAR_ACROSS)
+
+
+def slope(v):
+    s = sigmoid(v)
+    return s * (1.0 + v * (1.0 - s))
+
+
+def slab_rows(height):
+    return lambda ref, n: ref.at[pl.ds(pl.multiple_of(n * height, 16), height), :]
+
+
+def slab_cols(ref, n):
+    return ref.at[:, pl.ds(pl.multiple_of(n * 512, 512), 512)]
+
+
+def backward_kernel(
+    d_heads, new_head, hidden_out, pre_out, w_out, w_mix, residual, gain_all, hidden_in, pre_in,
+    tokens_in, normed_in,
+    sum_out, sum_mix, sum_in,
+    w_out_v, w_mix_v, tokens, normed, d_pre_out, d_pre_in, hidden_t, d_normed,
+    partial, twin_part, landing, arrived, gain_parts, gain_land,
+    whole_out, whole_mix, whole_in, land_out, land_mix, land_in, x_out, x_mix, x_in,
+    send_sems, recv_sems, local_sems,
+):
+    place = Place()
+    task = TaskPlace()
+    wires = Wires(send_sems, recv_sems)
+    me = place.me
+    get_out = load(w_out, w_out_v, local_sems, 0)
+    get_normed = load(normed_in, normed, local_sems, 1)
+    get_mix = load(w_mix, w_mix_v, local_sems, 2)
+    get_tokens = load(tokens_in, tokens, local_sems, 3)
+    greet_all(task)
+
+    d_hidden = dot(d_heads[...], new_head[...], ((1,), (1,)))
+    d_pre_out[...] = (d_hidden * slope(pre_out[...])).astype(BF16)
+    get_out.wait()
+    scatter = Scatter(place, wires, partial, twin_part, landing)
+    scatter.open(lambda half: wide_product(d_pre_out, w_out_v, partial, half, True))
+    for_out = TaskSum(task, wires, slab_rows(512), whole_out, land_out, x_out, sum_out)
+    for_mix = TaskSum(task, wires, slab_cols, whole_mix, land_mix, x_mix, sum_mix)
+    for_in = TaskSum(task, wires, slab_rows(528), whole_in, land_in, x_in, sum_in)
+
+    def tall_product(left, right, whole, height, dy):
+        k = plus(task.y, dy, 4)
+
+        def tile(n, carry):
+            feature = pl.multiple_of(k * 1024 + n * 256, 256)
+            at = pl.multiple_of((k * 2 + n // 2) * height + lax.rem(n, 2) * 256, 16)
+            value = dot(left[:, pl.ds(feature, 256)], right[...], ((0,), (0,)))
+            whole[pl.ds(at, 256), :] = value.astype(BF16)
+            return carry
+
+        lax.fori_loop(0, 4, tile, 0)
+
+    def mix_product(dy):
+        k = plus(task.y, dy, 4)
+
+        def tile(n, carry):
+            at = pl.multiple_of(k * 1024 + n * 256, 256)
+            whole_mix[:, pl.ds(at, 256)] = dot(hidden_t[...], arrived[:, pl.ds(at, 256)]).astype(BF16)
+            return carry
+
+        lax.fori_loop(0, 4, tile, 0)
+
+    def out_product(dy):
+        tall_product(normed, d_pre_out, whole_out, 512, dy)
+
+    def in_product(dy):
+        tall_product(tokens, d_pre_in, whole_in, 528, dy)
+
+    get_normed.wait()
+    out_product(2)
+    for_out.far()
+    scatter.finish_far()
+    out_product(1)
+    out_product(3)
+    for_out.near()
+    scatter.finish_across()
+    out_product(0)
+    scatter.finish_near()
+    hidden_t[...] = hidden_in[...].T
+    for_out.relay()
+
+    def store(half, value):
+        d_normed[:, half_cols(half)] = value
+
+    scatter.finish(store)
+    gain_rows = jnp.zeros((8, 4096), F32)
+    for m in range(2):
+        r = pl.ds(m * 16, 16)
+        v = residual[r, :]
+        inverse = lax.rsqrt(jnp.mean(v * v, axis=1, keepdims=True) + NORM_EPS)
+        d = d_normed[r, :]
+        scaled = d * gain_all[...]
+        inner = jnp.sum(scaled * v, axis=1, keepdims=True)
+        step = inverse * scaled - v * (inverse * inverse * inverse * inner * (1.0 / 4096))
+        arrived[pl.ds(pl.multiple_of(me * 32 + m * 16, 16), 16), :] = step.astype(BF16)
+        d_normed[r, :] = d * v * inverse
+    gather = Gather(place, wires, row_view(arrived))
+    gather.open()
+    for m in range(4):
+        gain_rows = gain_rows + d_normed[pl.ds(m * 8, 8), :]
+    for n in range(16):
+        gain_parts[n] = gain_rows[:, n * 256 : n * 256 + 256]
+    for_out.fold()
+    gain_slot = wires.claim(15)
+    for hop in range(1, 16):
+        peer = plus(me, hop, 16)
+        wires.send(gain_parts.at[peer], gain_land.at[hop - 1], gain_slot + hop - 1, peer)
+    gather.middle()
+    get_mix.wait()
+
+    def hidden_slab(dz):
+        rows = pl.ds(pl.multiple_of(plus(place.z, dz, 4) * 128, 128), 128)
+        d = dot(arrived[rows, :], w_mix_v[...], ((1,), (1,)))
+        d_pre_in[rows, :] = (d * slope(pre_in[rows, :])).astype(BF16)
+
+    gather.wait_twin(gather.OWN, gather.ACROSS)
+    hidden_slab(0)
+    gather.late()
+    for_out.finish()
+    gather.wait_twin(gather.FROM_UP, gather.UP_ACROSS)
+    hidden_slab(1)
+    gather.last()
+    gather.wait_twin(gather.FROM_DOWN, gather.DOWN_ACROSS)
+    hidden_slab(3)
+    gather.wait_twin(gather.FAR, gather.FAR_ACROSS)
+    mix_product(2)
+    for_mix.far()
+    hidden_slab(2)
+    mix_product(1)
+    mix_product(3)
+    for_mix.near()
+    for_out.spread()
+    mix_product(0)
+    get_tokens.wait()
+    in_product(2)
+    small = dot(d_heads[...], hidden_out[...], ((0,), (0,)))
+    bias = jnp.sum(d_heads[...].astype(F32), axis=0, keepdims=True)
+    gain_total = jnp.sum(gain_parts[me], axis=0, keepdims=True)
+    for hop in range(1, 16):
+        wires.arrived(gain_land.at[hop - 1], gain_slot + hop - 1)
+        gain_total = gain_total + jnp.sum(gain_land[hop - 1], axis=0, keepdims=True)
+    row = lax.broadcasted_iota(jnp.int32, (128, 256), 0)
+    bias = jnp.concatenate([bias, jnp.zeros((1, 128), F32)], axis=1)
+    small = jnp.where(row == 80, bias, jnp.where(row == 88, gain_total, small)).astype(BF16)
+    for n in range(8):
+        whole_in[pl.ds(n * 528 + 512, 16), :] = small[n * 16 : n * 16 + 16, :]
+    for_in.far()
+    in_product(1)
+    in_product(3)
+    for_in.near()
+    for_mix.relay()
+    in_product(0)
+    for_out.spread_far()
+    for_in.relay()
+    for_mix.fold()
+    for_out.end()
+    for_in.fold()
+    for_mix.finish()
+    for_mix.spread()
+    for_in.finish()
+    for_mix.spread_far()
+    for_in.spread()
+    for_mix.end()
+    for_in.spread_far()
+    for_in.end()
+    wires.drain()
+
+
+def hbm():
+    return pl.BlockSpec(memory_space=pltpu.HBM)
+
+
+def vmem():
+    return pl.BlockSpec(memory_space=pltpu.VMEM)
+
+
+def exchange_scratch():
+    return [
+        pltpu.VMEM((512, 4096), BF16),
+        pltpu.VMEM((8, 32, 4096), BF16),
+        pltpu.VMEM((7, 32, 4096), BF16),
+        pltpu.VMEM((512, 4096), BF16),
+    ]
+
+
+def parameters(collective_id):
+    return pltpu.CompilerParams(
+        collective_id=collective_id, has_side_effects=True, vmem_limit_bytes=62 * 2**20
+    )
+
+
+def forward_call(own_tokens, gain, w_in, w_mix):
+    return pl.pallas_call(
+        forward_kernel,
+        out_shape=[
+            jax.ShapeDtypeStruct((512, 4096), BF16),
+            jax.ShapeDtypeStruct((512, 256), F32),
+            jax.ShapeDtypeStruct((512, 256), BF16),
+            jax.ShapeDtypeStruct((32, 4096), F32),
+            jax.ShapeDtypeStruct((1, 4096), F32),
+            jax.ShapeDtypeStruct((512, 4096), BF16),
+        ],
+        in_specs=[hbm(), vmem(), hbm(), hbm()],
+        out_specs=[hbm(), vmem(), vmem(), vmem(), vmem(), hbm()],
+        scratch_shapes=[
+            pltpu.VMEM((528, 4096), BF16),
+            pltpu.VMEM((4096, 256), BF16),
+            pltpu.VMEM((256, 4096), BF16),
+            *exchange_scratch(),
+            pltpu.SemaphoreType.DMA((96,)),
+            pltpu.SemaphoreType.DMA((96,)),
+            pltpu.SemaphoreType.DMA((5,)),
+        ],
+        compiler_params=parameters(0),
+        name="forward",
+    )(own_tokens, gain, w_in, w_mix)
+
+
+def backward_call(
+    d_heads, new_head, hidden_out, pre_out, w_out, w_mix, residual, gain_all, hidden_in, pre_in,
+    tokens, normed,
+):
+    v, h = vmem(), hbm()
+    return pl.pallas_call(
+        backward_kernel,
+        out_shape=[
+            jax.ShapeDtypeStruct((4096, 256), BF16),
+            jax.ShapeDtypeStruct((256, 4096), BF16),
+            jax.ShapeDtypeStruct((4224, 256), BF16),
+        ],
+        in_specs=[v, v, v, v, h, h, v, v, v, v, h, h],
+        out_specs=[v, v, v],
+        scratch_shapes=[
+            pltpu.VMEM((4096, 256), BF16),
+            pltpu.VMEM((256, 4096), BF16),
+            pltpu.VMEM((512, 4096), BF16),
+            pltpu.VMEM((512, 4096), BF16),
+            pltpu.VMEM((512, 256), BF16),
+            pltpu.VMEM((512, 256), BF16),
+            pltpu.VMEM((256, 512), BF16),
+            pltpu.VMEM((32, 4096), F32),
+            *exchange_scratch(),
+            pltpu.VMEM((16, 8, 256), F32),
+            pltpu.VMEM((15, 8, 256), F32),
+            pltpu.VMEM((4096, 256), BF16),
+            pltpu.VMEM((256, 4096), BF16),
+            pltpu.VMEM((4224, 256), BF16),
+            pltpu.VMEM((3, 2, 512, 256), BF16),
+            pltpu.VMEM((3, 2, 256, 512), BF16),
+            pltpu.VMEM((3, 2, 528, 256), BF16),
+            pltpu.VMEM((512, 256), BF16),
+            pltpu.VMEM((256, 512), BF16),
+            pltpu.VMEM((528, 256), BF16),
+            pltpu.SemaphoreType.DMA((128,)),
+            pltpu.SemaphoreType.DMA((128,)),
+            pltpu.SemaphoreType.DMA((4,)),
+        ],
+        compiler_params=parameters(1),
+        name="backward",
+    )(
+        d_heads, new_head, hidden_out, pre_out, w_out, w_mix, residual, gain_all, hidden_in,
+        pre_in, tokens, normed,
+    )
 
 
 def sent_to_all(value, axis):
@@ -53,17 +828,6 @@
 def gathered_copies(value, axis, dim):
     parts = sent_to_all(value, axis)
     return joined_along(parts, dim)
-
-
-def summed_on_arrival(value, axis, dim):
-    parts = cut_along(value, dim, lax.axis_size(axis))
-    arrived = lax.all_to_all(parts, axis, split_axis=0, concat_axis=0, tiled=True)
-    return arrived.sum(axis=0)
-
-
-def silu_slope(before):
-    sigmoid = jax.nn.sigmoid(before)
-    return sigmoid * (1.0 + before * (1.0 - sigmoid))
 
 
 def discounted_sums(values, factors):
@@ -177,7 +941,6 @@
     groups = lax.axis_size("tp")
     full_width = part_width * groups
     row_count = env_count * frames
-    local_rows = row_count // groups
     own_tokens = observations.reshape(row_count, part_width)
     discount_factors = DISCOUNT * (1.0 - episode_ends.astype(jnp.float32))
     counts, totals, squares = popart_partials(task_indices, rewards, discount_factors)
@@ -189,25 +952,9 @@
         w_head, head_bias, pop_mean, pop_scale, updated_return_mean, updated_return_scale
     )
     loss_weighting = float(env_count * lax.axis_size("task")) ** (-0.5)
-    tokens, gain_all = (
-        lax.all_gather(own_tokens, "tp", axis=1, tiled=True),
-        lax.all_gather(gain.astype(jnp.bfloat16), "tp", axis=0, tiled=True).astype(gain.dtype),
-    )
-    row_offset = lax.axis_index("tp") * local_rows
-    token_rows = lax.dynamic_slice_in_dim(tokens, row_offset, local_rows, 0)
-    pre_in = jnp.dot(tokens, w_in, preferred_element_type=jnp.float32)
-    hidden_in = jax.nn.silu(pre_in).astype(jnp.bfloat16)
-    hidden_rows = hidden_in
-    mix_sum = lax.psum_scatter(
-        jnp.dot(hidden_rows, w_mix, preferred_element_type=jnp.float32).astype(jnp.bfloat16),
-        "tp",
-        scatter_dimension=0,
-        tiled=True,
-    ).astype(jnp.float32)
-    residual = token_rows.astype(jnp.float32) + mix_sum
-    inverse = lax.rsqrt(jnp.mean(residual * residual, axis=1, keepdims=True) + NORM_EPS)
-    normed = (residual * inverse * gain_all[None, :]).astype(jnp.bfloat16)
-    normed_all = lax.all_gather(normed, "tp", axis=0, tiled=True)
+    tokens, pre_in, hidden_in, residual, gain_all, normed_all = forward_call(
+        own_tokens, gain.reshape(1, part_width), w_in, w_mix
+    )
     pre_out = jnp.dot(normed_all, w_out, preferred_element_type=jnp.float32)
     hidden_out = jax.nn.silu(pre_out).astype(jnp.bfloat16)
     head_terms = jnp.dot(hidden_out, new_head, preferred_element_type=jnp.float32)
@@ -239,38 +986,28 @@
     (d_heads,) = pullback(jnp.ones((), jnp.float32))
     d_local = d_heads.reshape(env_share * frames, -1).astype(jnp.bfloat16)
     d_rounded = gathered_copies(d_local, "tp", 0)
-    grad_head = jnp.dot(hidden_out.T, d_rounded, preferred_element_type=jnp.float32)
-    grad_bias = jnp.sum(d_rounded.astype(jnp.float32), axis=0)
-    d_hidden_out = jnp.dot(d_rounded, new_head.T, preferred_element_type=jnp.float32)
-    d_pre_out = (d_hidden_out * silu_slope(pre_out)).astype(jnp.bfloat16)
-    grad_out = jnp.dot(normed_all.T, d_pre_out, preferred_element_type=jnp.float32)
-    d_normed = lax.psum_scatter(
-        jnp.dot(d_pre_out, w_out.T, preferred_element_type=jnp.float32).astype(jnp.bfloat16),
-        "tp",
-        scatter_dimension=0,
-        tiled=True,
-    ).astype(jnp.float32)
-    scaled = d_normed * gain_all[None, :]
-    inner_sum = jnp.sum(scaled * residual, axis=1, keepdims=True)
-    d_residual = (inverse * scaled - residual * inverse**3 * inner_sum / full_width).astype(
-        jnp.bfloat16
-    )
-    grad_gain = summed_on_arrival(jnp.sum(d_normed * residual * inverse, axis=0), "tp", 0)
-    arrived = lax.all_gather(d_residual, "tp", axis=0, tiled=True)
-    hidden_rows = hidden_in
-    grad_part = jnp.dot(hidden_rows.T, arrived, preferred_element_type=jnp.float32)
-    d_hidden = jnp.dot(arrived, w_mix.T, preferred_element_type=jnp.float32)
-    grad_mix = grad_part
-    d_pre_in = (d_hidden * silu_slope(pre_in)).astype(jnp.bfloat16)
-    grad_in = jnp.dot(tokens.T, d_pre_in, preferred_element_type=jnp.float32)
-    grad_in, grad_mix, grad_out, grad_gain, grad_head, grad_bias = (
-        lax.psum(grad_in.astype(jnp.bfloat16), "task").astype(jnp.float32),
-        lax.psum(grad_mix.astype(jnp.bfloat16), "task").astype(jnp.float32),
-        lax.psum(grad_out.astype(jnp.bfloat16), "task").astype(jnp.float32),
-        lax.psum(grad_gain.astype(jnp.bfloat16), "task").astype(jnp.float32),
-        lax.psum(grad_head.astype(jnp.bfloat16), "task").astype(jnp.float32),
-        lax.psum(grad_bias.astype(jnp.bfloat16), "task").astype(jnp.float32),
-    )
+    pad = ((0, 0), (0, 128 - d_rounded.shape[1]))
+    sum_out, sum_mix, sum_in = backward_call(
+        jnp.pad(d_rounded, pad),
+        jnp.pad(new_head, pad),
+        hidden_out,
+        pre_out,
+        w_out,
+        w_mix,
+        residual,
+        gain_all,
+        hidden_in,
+        pre_in,
+        tokens,
+        normed_all,
+    )
+    sum_in = sum_in.reshape(8, 528, part_width)
+    grad_in = sum_in[:, :512].astype(jnp.float32).reshape(full_width, part_width)
+    small = sum_in[:, 512:].astype(jnp.float32).reshape(128, part_width)
+    grad_head = small[: ACTIONS + TASKS].T
+    grad_bias = small[80, : ACTIONS + TASKS]
+    grad_gain = small[88]
+    grad_out, grad_mix = sum_out.astype(jnp.float32), sum_mix.astype(jnp.float32)
     return (
         grad_in,
         grad_mix,

time: 499 us -> 289 us (0.58)
  waiting for transfers between devices: 339 us -> 10.9 us
  Pallas kernels: 0 us -> 219 us
  blocking collectives: 66.7 us -> 0 us
  matrix products: 37 us -> 7.08 us
  between operations: 14.4 us -> 0.87 us
    pallas_call x0 -> x2, Pallas kernels: none -> 219 us  [the longest x1 146 us: backward_call(): pl.pallas_call(backward_kernel, out_shape=[jax.ShapeDtypeStruct((4096, 25...]
    reduce_scatter x2 -> x0, waiting for transfers between devices: 116 us -> none  [the longest x1 67 us: on_device(): lax.psum_scatter(jnp.dot(d_pre_out, w_out.T, preferred_element_type=jnp.f...]
    all_gather x3 -> x0, waiting for transfers between devices: 108 us -> none  [the longest x1 50.4 us: on_device(): lax.all_gather(own_tokens, 'tp', axis=1, tiled=True)]
    psum x1 -> x0, waiting for transfers between devices: 96.4 us -> none  [on_device(): lax.psum(grad_in.astype(jnp.bfloat16), 'task').astype(jnp.float32)]
    psum x1 -> x0, blocking collectives: 38.7 us -> none  [on_device(): lax.psum(grad_gain.astype(jnp.bfloat16), 'task').astype(jnp.float32)]
    dot_general x8 -> x0, matrix products: 31.3 us -> none  [the longest x1 9.4 us: on_device(): grad_in = jnp.dot(tokens.T, d_pre_in, preferred_element_type=jnp.float32)]
    all_gather x1 -> x0, blocking collectives: 18.6 us -> none  [on_device(): lax.all_gather(gain.astype(jnp.bfloat16), 'tp', axis=0, tiled=True)]
    add x30, other arithmetic: 0.56 us -> 10.9 us  [advance(): latest = column[0] + column[1] * running]
  transfers between devices with their start and end apart: 9 -> 3, of which waited for: 9 -> 2; matrix products, arithmetic and copies ran while one was open for 2% -> 3% of each run, Pallas kernels for 0% -> 25%
where the time goes in v1:
time: 289 us; the launch traced here: 287 us
  Pallas kernels  219 us (76%)
  other arithmetic  20.4 us (7%)
  starting transfers between devices  15.4 us (5%)
  local copies, waits for them, and re-layouts  12.9 us (4%)
  waiting for transfers between devices  10.9 us (4%)
  matrix products  7.08 us (2%)
    pallas_call x1, Pallas kernels, backward_call(): pl.pallas_call(backward_kernel, out_shape=[jax.ShapeDtypeStruct((4096, 25...  146 us
    pallas_call x1, Pallas kernels, forward_call(): pl.pallas_call(forward_kernel, out_shape=[jax.ShapeDtypeStruct((512, 4096...  73 us
    all_to_all x2, starting transfers between devices, sent_to_all(): return lax.all_to_all(copies, axis, split_axis=0, concat_axis=0, tiled=True)  11.4 us
    add x30, other arithmetic, advance(): latest = column[0] + column[1] * running  10.9 us
    all_to_all x1, waiting for transfers between devices, sum_at_owner(): lax.all_to_all(parts, axis, split_axis=0, concat_axis=0, tiled=True)  6.03 us
  transfers between devices with their start and end apart: 3, of which 2 were waited for; matrix products, arithmetic and copies ran while one was open for 3% of the time, Pallas kernels for 25%

profile of v1, /device:TPU:1, one launch (start us, length us, event | category | flops | bytes accessed | tf_op | source)
XLA Modules:
  0.0 287.2 jit_solution(4648351377662779711)
XLA Ops:
  0.7 0.7 convert_reduce_fusion.1
  1.4 0.8 copy.62
  2.3 11.1 %while.34 = (s32[]{:T(128)}, f32[32]{0:T(128)S(1)}, f32[15,32]{1,0:T(8,128)S(1)}, f32[15,32]{1,0:T(8,128)}, f32[15,32]{1,0:T(8,128)S(1)}, /*index=5*/s32[]{:T(128)}, s32[]{:T(128)}, s32[]{:T(128)}) while((s32[]{:T(128)}, f32[32]{0:T(128)S(1)}, f32[15,32]{1,0:T(8,128)S(1)}, f32[15,32]{1,0:T(8,128)}, f32[15,32]{1,0:T(8,128)S(1)}, ...), condition=%wide.region_2.3_spmd.clone, body=%wide.region_1.2_spmd.clone.sunk | while | flops 100 | bytes 891 | solution.py:840
  5.2 0.7 fusion.40
  13.4 0.8 convolution_bitcast_fusion.3
  14.2 0.8 convolution_bitcast_fusion.2
  15.6 7.5 %all-to-all-start = ((f32[8,1,171]{2,1,0:T(1,128)}), f32[8,1,171]{2,1,0:T(1,128)S(1)}, u32[]{:S(2)}, u32[]{:S(2)}) async-start(f32[8,1,171]{2,1,0:T(1,128)} %broadcast_in_dim.68), calls=%async_computation | async-start | bytes 16384 | tf_op jit(solution)/shard_map/all_to_all | solution.py:794
  23.1 0.7 dynamic_slice.53
  23.9 0.8 constant_dynamic-slice_fusion.1
  24.7 73.0 %forward.1 = (bf16[512,4096]{1,0:T(8,128)(2,1)}, f32[512,256]{1,0:T(8,128)}, bf16[512,256]{1,0:T(8,128)(2,1)}, f32[32,4096]{1,0:T(8,128)}, f32[1,4096]{1,0:T(1,128)}, /*index=5*/bf16[512,4096]{1,0:T(8,128)(2,1)}) custom-call(bf16[512,256]{1,0:T(8,128)(2,1)} %bitcast.96, f32[1,256]{1,0:T(1,128)} %bitcast.103, bf16[4096,256]{1,0:T(8,128)(2,1)} %w_in.1, ...), custom_call_target="tpu_custom_call" | custom-call | tf_op jit(solution)/shard_map/forward/pallas_call | solution.py:719
  97.7 4.9 %multiply_convert_fusion = (bf16[512,256]{1,0:T(8,128)(2,1)S(1)}, f32[512,256]{1,0:T(8,128)}) fusion(bf16[512,4096]{1,0:T(8,128)(2,1)} %get-tuple-element.225.normed_in, bf16[4096,256]{1,0:T(8,128)(2,1)} %w_out.1), kind=kOutput, calls=%fused_computation.12 | convolution fusion | flops 1074397184 | bytes 7077888 | tf_op jit(solution)/shard_map/dot_general | solution.py:958
  104.0 0.8 copy.65
  104.8 4.0 %all-to-all-start.1 = ((bf16[16,32,75]{2,1,0:T(8,128)(2,1)}), bf16[16,32,75]{2,1,0:T(8,128)(2,1)S(1)}, u32[]{:S(2)}, u32[]{:S(2)}) async-start(bf16[16,32,75]{2,1,0:T(8,128)(2,1)} %bitcast.8), calls=%async_computation.1 | async-start | bytes 262144 | tf_op jit(solution)/shard_map/all_to_all | solution.py:818
  108.9 6.0 %all-to-all-done.1 = bf16[16,32,75]{2,1,0:T(8,128)(2,1)S(1)} async-done(((bf16[16,32,75]{2,1,0:T(8,128)(2,1)}), bf16[16,32,75]{2,1,0:T(8,128)(2,1)S(1)}, u32[]{:S(2)}, u32[]{:S(2)}) %all-to-all-start.1) | async-done | bytes 76832 | tf_op jit(solution)/shard_map/all_to_all | solution.py:818
  115.8 1.1 while.35
  118.2 4.0 %all-to-all-start.2 = ((bf16[16,32,75]{2,1,0:T(8,128)(2,1)}), bf16[16,32,75]{2,1,0:T(8,128)(2,1)S(1)}, u32[]{:S(2)}, u32[]{:S(2)}) async-start(bf16[16,32,75]{2,1,0:T(8,128)(2,1)} %broadcast_in_dim.75), calls=%async_computation.2 | async-start | bytes 262144 | tf_op jit(solution)/shard_map/all_to_all | solution.py:794
  122.2 0.7 copy.72
  123.5 4.8 %all-to-all-done.2 = bf16[16,32,75]{2,1,0:T(8,128)(2,1)S(1)} async-done(((bf16[16,32,75]{2,1,0:T(8,128)(2,1)}), bf16[16,32,75]{2,1,0:T(8,128)(2,1)S(1)}, u32[]{:S(2)}, u32[]{:S(2)}) %all-to-all-start.2) | async-done | bytes 76832 | tf_op jit(solution)/shard_map/all_to_all | solution.py:794
  129.0 146.5 %backward.1 = (bf16[4096,256]{1,0:T(8,128)(2,1)}, bf16[256,4096]{1,0:T(8,128)(2,1)}, bf16[4224,256]{1,0:T(8,128)(2,1)}) custom-call(bf16[512,128]{1,0:T(8,128)(2,1)} %pad.21.d_heads, bf16[256,128]{1,0:T(8,128)(2,1)} %pad.22.new_head, bf16[512,256]{1,0:T(8,128)(2,1)} %copy-done.3, f32[512,256]{1,0:T(8,128)} %get-tuple-element.389.pre_out, ...), custom_call_target="tpu_custom_call" | custom-call | tf_op jit(solution)/shard_map/backward/pallas_call | solution.py:750
  275.6 0.9 slice.73
  276.4 1.7 slice.72
  279.9 2.5 bitcast_convert_fusion
  282.4 2.5 convert_element_type.56
  284.9 2.3 convert_element_type.57
  (134 shorter events, 18.7 us)
Async XLA Ops:
  0.6 102.0 %copy-start = (s32[32,15]{0,1:T(8,128)S(1)}, s32[32,15]{0,1:T(8,128)}, u32[]{:S(2)}) copy-start(s32[32,15]{0,1:T(8,128)} %param.28) | copy-start | bytes 5764
  15.6 87.5 %all-to-all-start = ((f32[8,1,171]{2,1,0:T(1,128)}), f32[8,1,171]{2,1,0:T(1,128)S(1)}, u32[]{:S(2)}, u32[]{:S(2)}) async-start(f32[8,1,171]{2,1,0:T(1,128)} %broadcast_in_dim.68), calls=%async_computation | async-start | bytes 16384 | tf_op jit(solution)/shard_map/all_to_all | solution.py:794
  97.7 5.3 %copy-start.4 = (bf16[256,75]{0,1:T(8,128)(2,1)S(1)}, bf16[256,75]{0,1:T(8,128)(2,1)}, u32[]{:S(2)}) copy-start(bf16[256,75]{0,1:T(8,128)(2,1)} %param.23) | copy-start | bytes 115204
  97.7 5.5 %copy-start.6 = (f32[57]{0:T(128)S(1)}, f32[57]{0:T(128)}, u32[]{:S(2)}) copy-start(f32[57]{0:T(128)} %param.25) | copy-start | bytes 688
  97.7 5.5 %copy-start.7 = (f32[57]{0:T(128)S(1)}, f32[57]{0:T(128)}, u32[]{:S(2)}) copy-start(f32[57]{0:T(128)} %param.26) | copy-start | bytes 688
  97.7 5.5 %copy-start.8 = (f32[75]{0:T(128)S(1)}, f32[75]{0:T(128)}, u32[]{:S(2)}) copy-start(f32[75]{0:T(128)} %param.24) | copy-start | bytes 904
  102.6 26.4 %copy-start.3 = (bf16[512,256]{1,0:T(8,128)(2,1)}, bf16[512,256]{1,0:T(8,128)(2,1)S(1)}, u32[]{:S(2)}) copy-start(bf16[512,256]{1,0:T(8,128)(2,1)S(1)} %get-tuple-element.388.hidden_out) | copy-start | bytes 786436
  103.3 172.3 %copy-start.9 = (f32[57]{0:T(128)}, f32[57]{0:T(128)S(1)}, u32[]{:S(2)}) copy-start(f32[57]{0:T(128)S(1)} %get-tuple-element.384) | copy-start | bytes 688
  103.3 172.3 %copy-start.10 = (f32[57]{0:T(128)}, f32[57]{0:T(128)S(1)}, u32[]{:S(2)}) copy-start(f32[57]{0:T(128)S(1)} %get-tuple-element.385) | copy-start | bytes 688
  104.8 10.1 %all-to-all-start.1 = ((bf16[16,32,75]{2,1,0:T(8,128)(2,1)}), bf16[16,32,75]{2,1,0:T(8,128)(2,1)S(1)}, u32[]{:S(2)}, u32[]{:S(2)}) async-start(bf16[16,32,75]{2,1,0:T(8,128)(2,1)} %bitcast.8), calls=%async_computation.1 | async-start | bytes 262144 | tf_op jit(solution)/shard_map/all_to_all | solution.py:818
  108.9 166.7 %copy-start.5 = (f32[75]{0:T(128)}, f32[75]{0:T(128)S(1)}, u32[]{:S(2)}) copy-start(f32[75]{0:T(128)S(1)} %pad_maximum_fusion.1) | copy-start | bytes 904
  118.2 10.2 %all-to-all-start.2 = ((bf16[16,32,75]{2,1,0:T(8,128)(2,1)}), bf16[16,32,75]{2,1,0:T(8,128)(2,1)S(1)}, u32[]{:S(2)}, u32[]{:S(2)}) async-start(bf16[16,32,75]{2,1,0:T(8,128)(2,1)} %broadcast_in_dim.75), calls=%async_computation.2 | async-start | bytes 262144 | tf_op jit(solution)/shard_map/all_to_all | solution.py:794
  279.9 2.5 copy-start.2
  282.4 2.5 copy-start.1

commit v2 on v1

v2 whole, which is shorter than its diff:
```python
import jax
import jax.numpy as jnp
from jax import lax
from jax.experimental import pallas as pl
from jax.experimental.pallas import tpu as pltpu
from jax.sharding import PartitionSpec as P

ACTIONS = 18
TASKS = 57
DISCOUNT = 0.99
BASELINE_COST = 0.5
ENTROPY_COST = 0.01
POPART_PRIOR = 64.0
NORM_EPS = 1e-06
LOSS_WEIGHT = 256**-0.5
SENDS = 248
RECEIVES = 248


MESH = pl.DeviceIdType.MESH
F32 = jnp.float32
BF16 = jnp.bfloat16
HALVES = (0, 1)


def plus(a, b, n):
    return lax.rem(a + b, n)


class Place:
    def __init__(self):
        self.me = lax.axis_index("tp")
        self.z = self.me // 4
        self.x = lax.rem(self.me // 2, 2)
        self.c = lax.rem(self.me, 2)
        self.across = self.at(0, 1)
        self.up = self.at(1, 0)
        self.down = self.at(3, 0)
        self.partner = self.at(0, 0, 1)

    def at(self, dz, dx, dc=0):
        return (plus(self.z, dz, 4) * 2 + plus(self.x, dx, 2)) * 2 + plus(self.c, dc, 2)


class Wires:
    def __init__(self, send_sems, recv_sems):
        self.send_sems = send_sems
        self.recv_sems = recv_sems
        self.sent = []
        self.drained = 0
        self.slots = 0

    def claim(self, count):
        first = self.slots
        self.slots += count
        return first

    def send(self, src, dst, slot, peer, axis="tp"):
        copy = pltpu.make_async_remote_copy(
            src_ref=src,
            dst_ref=dst,
            send_sem=self.send_sems.at[len(self.sent)],
            recv_sem=self.recv_sems.at[slot],
            device_id={axis: peer},
            device_id_type=MESH,
        )
        copy.start()
        self.sent.append(copy)

    def arrived(self, dst, slot, axis="tp"):
        pltpu.make_async_remote_copy(
            src_ref=dst,
            dst_ref=dst,
            send_sem=self.send_sems.at[0],
            recv_sem=self.recv_sems.at[slot],
            device_id={axis: lax.axis_index(axis)},
            device_id_type=MESH,
        ).wait_recv()

    def drain_all_but(self, last):
        for copy in self.sent[: len(self.sent) - last]:
            copy.wait_send()
        self.drained = len(self.sent) - last

    def drain(self):
        for copy in self.sent[self.drained :]:
            copy.wait_send()


class Gather:
    ACROSS, FROM_DOWN, FROM_UP, DOWN_ACROSS, UP_ACROSS, FAR, FAR_ACROSS, OWN = range(8)

    def __init__(self, place, wires, view):
        self.place = place
        self.wires = wires
        self.view = view
        self.first = wires.claim(30)
        p = place
        self.block = {
            self.ACROSS: p.at(0, 1),
            self.FROM_DOWN: p.at(3, 0),
            self.FROM_UP: p.at(1, 0),
            self.DOWN_ACROSS: p.at(3, 1),
            self.UP_ACROSS: p.at(1, 1),
            self.FAR: p.at(2, 0),
            self.FAR_ACROSS: p.at(2, 1),
            self.OWN: p.me,
        }
        self.twin = {k: plus(b, 0, 16) + 1 - 2 * p.c for k, b in self.block.items()}

    def slot(self, kind, half):
        return self.first + kind * 2 + half

    def twin_slot(self, kind, half):
        return self.first + 14 + kind * 2 + half

    def pass_on(self, kind, half, peer, kind_there):
        v = self.view(self.block[kind], half)
        self.wires.send(v, v, self.slot(kind_there, half), peer)

    def to_twin(self, kind, half):
        v = self.view(self.block[kind], half)
        self.wires.send(v, v, self.twin_slot(kind, half), self.place.partner)

    def wait(self, kind, half):
        self.wires.arrived(self.view(self.block[kind], half), self.slot(kind, half))

    def wait_twin(self, *kinds):
        for kind in kinds:
            for half in HALVES:
                self.wires.arrived(
                    self.view(self.twin[kind], half), self.twin_slot(kind, half)
                )

    def open(self):
        p = self.place
        for half in HALVES:
            self.pass_on(self.OWN, half, p.up, self.FROM_DOWN)
            self.pass_on(self.OWN, half, p.down, self.FROM_UP)
            self.pass_on(self.OWN, half, p.across, self.ACROSS)
            self.to_twin(self.OWN, half)

    def middle(self):
        p = self.place
        self.wait(self.FROM_DOWN, 0)
        self.pass_on(self.FROM_DOWN, 0, p.up, self.FAR)
        self.to_twin(self.FROM_DOWN, 0)
        self.wait(self.FROM_UP, 0)
        self.to_twin(self.FROM_UP, 0)
        self.wait(self.ACROSS, 0)
        self.pass_on(self.ACROSS, 0, p.down, self.UP_ACROSS)
        self.wait(self.FROM_UP, 1)
        self.pass_on(self.FROM_UP, 1, p.down, self.FAR)
        self.pass_on(self.ACROSS, 0, p.up, self.DOWN_ACROSS)
        self.to_twin(self.ACROSS, 0)
        self.to_twin(self.FROM_UP, 1)
        self.wait(self.FROM_DOWN, 1)
        self.to_twin(self.FROM_DOWN, 1)
        self.wait(self.ACROSS, 1)
        self.pass_on(self.ACROSS, 1, p.up, self.DOWN_ACROSS)
        self.pass_on(self.ACROSS, 1, p.down, self.UP_ACROSS)
        self.to_twin(self.ACROSS, 1)
        for half in HALVES:
            self.wait(self.FAR, half)
            self.pass_on(self.FAR, half, p.across, self.FAR_ACROSS)
            self.to_twin(self.FAR, half)

    def late(self):
        for half in HALVES:
            for kind in (self.DOWN_ACROSS, self.UP_ACROSS):
                self.wait(kind, half)
                self.to_twin(kind, half)

    def last(self):
        for half in HALVES:
            self.wait(self.FAR_ACROSS, half)
            self.to_twin(self.FAR_ACROSS, half)


def half_cols(half):
    return pl.ds(half * 2048, 2048)


class Scatter:
    G, D, E, F, A, B, C = range(7)
    ORDER = ((2, 1), (1, 1), (3, 1), (1, 0), (3, 0), (2, 0), (0, 1), (0, 0))

    def __init__(self, place, wires, partial, twin_part, landing):
        self.place = place
        self.wires = wires
        self.partial = partial
        self.twin_part = twin_part
        self.landing = landing
        self.first = wires.claim(30)

    def rows(self, where, dc=0):
        return pl.ds(pl.multiple_of(self.place.at(*where, dc) * 32, 32), 32)

    def mine(self, where, half):
        return self.partial.at[self.rows(where), half_cols(half)]

    def twins(self, where, half):
        return self.twin_part.at[self.ORDER.index(where), :, half_cols(half)]

    def land(self, kind, half):
        return self.landing.at[kind, :, half_cols(half)]

    def total(self, where, half, kinds=(), waited=()):
        slot = self.first + 14 + self.ORDER.index(where) * 2 + half
        if (where, half) not in self.seen:
            self.wires.arrived(self.twins(where, half), slot)
            self.seen.add((where, half))
        for kind in kinds:
            self.wires.arrived(self.land(kind, half), self.first + kind * 2 + half)
        value = self.mine(where, half)[...].astype(F32) + self.twins(where, half)[...].astype(F32)
        for kind in kinds:
            value = value + self.land(kind, half)[...].astype(F32)
        return value

    def forward(self, where, half, kinds, peer, kind_there):
        self.mine(where, half)[...] = self.total(where, half, kinds).astype(BF16)
        self.wires.send(
            self.mine(where, half),
            self.land(kind_there, half),
            self.first + kind_there * 2 + half,
            peer,
        )

    def open(self, produce):
        self.seen = set()
        p = self.place
        for half in HALVES:
            produce(half)
            for where in self.ORDER:
                self.wires.send(
                    self.partial.at[self.rows(where, 1), half_cols(half)],
                    self.twins(where, half),
                    self.first + 14 + self.ORDER.index(where) * 2 + half,
                    p.partner,
                )
            self.forward((2, 1), half, (), p.across, self.G)
            self.forward((1, 1), half, (), p.up, self.D)
            self.forward((3, 1), half, (), p.down, self.E)
        self.forward((1, 0), 1, (), p.up, self.B)
        self.forward((3, 0), 0, (), p.down, self.C)

    def finish_far(self):
        p = self.place
        self.forward((2, 0), 0, (self.G,), p.up, self.F)
        self.forward((2, 0), 1, (self.G,), p.down, self.F)

    def finish_across(self):
        for half in HALVES:
            self.forward((0, 1), half, (self.D, self.E), self.place.across, self.A)

    def finish_near(self):
        p = self.place
        self.forward((1, 0), 0, (self.F,), p.up, self.B)
        self.forward((3, 0), 1, (self.F,), p.down, self.C)

    def finish(self, store):
        for half in HALVES:
            store(half, self.total((0, 0), half, (self.A, self.B, self.C)))


def sigmoid(v):
    return 1.0 / (1.0 + jnp.exp(-v))


def dot(a, b, contract=((1,), (0,))):
    return lax.dot_general(a, b, (contract, ((), ())), preferred_element_type=F32)


def load(src, dst, sems, at):
    copy = pltpu.make_async_copy(src, dst, sems.at[at])
    copy.start()
    return copy


def wide_product(left, right, partial, half, transposed):
    def tile(n, carry):
        at = pl.multiple_of(half * 2048 + n * 256, 256)
        if transposed:
            value = dot(left[...], right[pl.ds(at, 256), :], ((1,), (1,)))
        else:
            value = dot(left[...], right[:, pl.ds(at, 256)])
        partial[:, pl.ds(at, 256)] = value.astype(BF16)
        return carry

    lax.fori_loop(0, 8, tile, 0)


def row_view(ref):
    return lambda block, half: ref.at[
        pl.ds(pl.multiple_of(block * 32, 32), 32), half_cols(half)
    ]


class TaskPlace:
    def __init__(self):
        task = lax.axis_index("task")
        self.xh = task // 4
        self.y = lax.rem(task, 4)
        self.up = self.xh * 4 + plus(self.y, 1, 4)
        self.down = self.xh * 4 + plus(self.y, 3, 4)
        self.across = (1 - self.xh) * 4 + self.y


class TaskSum:
    F, B, C = range(3)
    OWN, FROM_DOWN, FROM_UP, DOWN_ACROSS, UP_ACROSS, FAR, FAR_ACROSS = range(7)

    def __init__(self, place, wires, view, whole, land, land_x, result):
        self.place = place
        self.wires = wires
        self.view = view
        self.whole = whole
        self.land = land
        self.land_x = land_x
        self.result = result
        self.first = wires.claim(14)

    def slab(self, ref, dy, part):
        return self.view(ref, plus(self.place.y, dy, 4) * 2 + part)

    def post(self, src, dst, slot, peer):
        self.wires.send(src, dst, self.first + slot, peer, "task")

    def wait(self, dst, slot):
        self.wires.arrived(dst, self.first + slot, "task")

    def far(self):
        p = self.place
        self.post(self.slab(self.whole, 2, 0), self.land.at[self.F, 0], 0, p.up)
        self.post(self.slab(self.whole, 2, 1), self.land.at[self.F, 1], 1, p.down)

    def near(self):
        p = self.place
        self.post(self.slab(self.whole, 1, 1), self.land.at[self.B, 1], 3, p.up)
        self.post(self.slab(self.whole, 3, 0), self.land.at[self.C, 0], 4, p.down)

    def relay(self):
        p = self.place
        for dy, part, kind, slot, peer in ((1, 0, self.B, 2, p.up), (3, 1, self.C, 5, p.down)):
            self.wait(self.land.at[self.F, part], part)
            own = self.slab(self.whole, dy, part)
            total = own[...].astype(F32) + self.land[self.F, part].astype(F32)
            own[...] = total.astype(BF16)
            self.post(own, self.land.at[kind, part], slot, peer)

    def local(self, part):
        return (
            self.slab(self.whole, 0, part)[...].astype(F32)
            + self.land[self.B, part].astype(F32)
            + self.land[self.C, part].astype(F32)
        )

    def fold(self):
        for kind, part, slot in ((self.B, 1, 3), (self.C, 0, 4), (self.B, 0, 2), (self.C, 1, 5)):
            self.wait(self.land.at[kind, part], slot)
        other = 1 - self.place.xh
        away = self.slab(self.whole, 0, other)
        away[...] = self.local(other).astype(BF16)
        self.post(away, self.land_x, 6, self.place.across)

    def pass_on(self, kind, peer, kind_there):
        v = self.held(kind)
        self.post(v, v, 6 + kind_there, peer)

    def held(self, kind):
        dy, across = {
            self.OWN: (0, 0),
            self.FROM_DOWN: (3, 0),
            self.FROM_UP: (1, 0),
            self.DOWN_ACROSS: (3, 1),
            self.UP_ACROSS: (1, 1),
            self.FAR: (2, 0),
            self.FAR_ACROSS: (2, 1),
        }[kind]
        xh = self.place.xh
        return self.slab(self.result, dy, 1 - xh if across else xh)

    def across_held(self):
        return self.slab(self.result, 0, 1 - self.place.xh)

    def finish(self):
        p = self.place
        self.wait(self.land_x, 6)
        own = self.held(self.OWN)
        own[...] = (self.local(p.xh) + self.land_x[...].astype(F32)).astype(BF16)
        self.post(own, own, 13, p.across)
        self.pass_on(self.OWN, p.up, self.FROM_DOWN)
        self.pass_on(self.OWN, p.down, self.FROM_UP)

    def get(self, kind):
        self.wait(self.held(kind), 6 + kind)

    def spread(self):
        p = self.place
        self.get(self.FROM_DOWN)
        self.pass_on(self.FROM_DOWN, p.up, self.FAR)
        self.get(self.FROM_UP)
        v = self.across_held()
        self.wait(v, 13)
        self.post(v, v, 6 + self.DOWN_ACROSS, p.up)
        self.post(v, v, 6 + self.UP_ACROSS, p.down)

    def spread_far(self):
        self.get(self.UP_ACROSS)
        self.pass_on(self.UP_ACROSS, self.place.down, self.FAR_ACROSS)
        self.get(self.DOWN_ACROSS)

    def end(self):
        self.get(self.FAR)
        self.get(self.FAR_ACROSS)


def slope(v):
    s = sigmoid(v)
    return s * (1.0 + v * (1.0 - s))


def slab_rows(height):
    return lambda ref, n: ref.at[pl.ds(pl.multiple_of(n * height, 16), height), :]


def slab_cols(ref, n):
    return ref.at[:, pl.ds(pl.multiple_of(n * 512, 512), 512)]


def popart_update(counts, totals, squares, pop_mean, pop_scale):
    mixing = counts / (counts + POPART_PRIOR)
    safe_counts = jnp.maximum(counts, 1.0)
    batch_mean = totals / safe_counts
    batch_square = squares / safe_counts
    updated_return_mean = (1.0 - mixing) * pop_mean + mixing * batch_mean
    mean_gap = batch_mean - pop_mean
    variance = (
        (1.0 - mixing) * pop_scale * pop_scale
        + mixing * (batch_square - batch_mean * batch_mean)
        + mixing * (1.0 - mixing) * mean_gap * mean_gap
    )
    return (updated_return_mean, jnp.sqrt(variance))


class AllPairs:
    def __init__(self, wires, axis, size, land):
        self.wires = wires
        self.axis = axis
        self.size = size
        self.here = lax.axis_index(axis)
        self.land = land
        self.first = wires.claim(size - 1)

    def post(self, peer_at, src):
        peer = plus(self.here, peer_at, self.size)
        self.wires.send(
            src(peer), self.land.at[peer_at - 1], self.first + peer_at - 1, peer, self.axis
        )

    def wait(self, peer_at):
        self.wires.arrived(self.land.at[peer_at - 1], self.first + peer_at - 1, self.axis)


def greet_everyone():
    barrier = pltpu.get_barrier_semaphore()
    for axis, size in (("tp", 16), ("task", 8)):
        here = lax.axis_index(axis)
        for hop in range(1, size):
            pl.semaphore_signal(
                barrier, inc=1, device_id={axis: plus(here, hop, size)}, device_id_type=MESH
            )
    pl.semaphore_wait(barrier, 22)


def lanes(shape):
    return lax.broadcasted_iota(jnp.int32, shape, 1)


def sublanes(shape):
    return lax.broadcasted_iota(jnp.int32, shape, 0)


def popart_rows(tasks, rewards, ends):
    factors = DISCOUNT * (1.0 - ends[...].astype(F32))
    gains = rewards[...]
    running = jnp.zeros((1, 32), F32)
    total = jnp.zeros((1, 32), F32)
    square = jnp.zeros((1, 32), F32)
    for t in range(14, -1, -1):
        running = gains[t : t + 1, :] + factors[t : t + 1, :] * running
        total = total + running
        square = square + running * running
    member = sublanes((128, 32)) == tasks[...] + ACTIONS
    diagonal = sublanes((128, 128)) == lanes((128, 128))
    rows = []
    for value in (jnp.full((1, 32), 15.0, F32), total, square):
        column = jnp.sum(jnp.where(member, value, 0.0), axis=1, keepdims=True)
        rows.append(jnp.sum(jnp.where(diagonal, column, 0.0), axis=0, keepdims=True))
    return jnp.concatenate([*rows, jnp.zeros((5, 128), F32)], axis=0)


def as_column(row):
    diagonal = sublanes((128, 128)) == lanes((128, 128))
    return jnp.sum(jnp.where(diagonal, row, 0.0), axis=1, keepdims=True)


def step_columns(ref, first_env):
    value = ref[...].astype(F32)
    value = jnp.concatenate([value, jnp.zeros((1, 32), F32)], axis=0)
    lane = lanes((16, 32))
    return jnp.concatenate(
        [
            jnp.sum(jnp.where(lane == first_env + e, value, 0.0), axis=1, keepdims=True)
            for e in (0, 1)
        ],
        axis=0,
    )


def loss_gradient(outputs, own, columns, mean, scale):
    action, reward, factor, behaviour = columns
    shape = (32, 128)
    lane = lanes(shape)
    frame = lax.rem(sublanes(shape), 16)
    live = frame < 15

    def later(value, by):
        return jnp.where(frame + by < 16, pltpu.roll(value, 32 - by, 0), 0.0)

    def over_lanes(mask, value):
        return jnp.broadcast_to(
            jnp.sum(jnp.where(mask, value, 0.0), axis=1, keepdims=True), shape
        )

    is_logit = lane < ACTIONS
    chosen = lane == action.astype(jnp.int32)
    log_total = jnp.log(over_lanes(is_logit, jnp.exp(jnp.where(is_logit, outputs, 0.0))))
    log_prob = jnp.where(is_logit, outputs - log_total, 0.0)
    log_policy = over_lanes(chosen, log_prob)
    env_mean = over_lanes(own, mean)
    env_scale = over_lanes(own, scale)
    norm_values = over_lanes(own, outputs)
    values = norm_values * env_scale + env_mean
    clipped = jnp.minimum(jnp.exp(log_policy - behaviour), 1.0)
    total = jnp.where(live, clipped * (reward + factor * later(values, 1) - values), 0.0)
    decay = jnp.where(live, factor * clipped, 0.0)
    for by in (1, 2, 4, 8):
        total = total + decay * later(total, by)
        decay = decay * later(decay, by)
    targets = values + total
    following = later(targets, 1)
    advantage = clipped * ((reward + factor * following - env_mean) / env_scale - norm_values)
    normed_targets = (targets - env_mean) / env_scale
    policy = jnp.where(is_logit, jnp.exp(log_prob), 0.0)
    entropy = -over_lanes(is_logit, policy * log_prob)
    d_logits = -advantage * (jnp.where(chosen, 1.0, 0.0) - policy) + ENTROPY_COST * policy * (
        log_prob + entropy
    )
    d_value = -BASELINE_COST * (normed_targets - norm_values)
    d = jnp.where(is_logit, d_logits, jnp.where(own, d_value, 0.0))
    return jnp.where(live, d * LOSS_WEIGHT, 0.0)


def step_kernel(
    own_tokens, gain, w_in, w_mix, w_out, head, vectors, tasks, actions, rewards, ends, behaviour,
    sum_out_hbm, sum_mix_hbm, sum_in_hbm, new_head, stats,
    tokens, w_in_v, w_mix_v, w_out_v, pre_in, hidden_in, residual, gain_all, normed,
    pre_out, hidden_out, head_part, head_land, d_heads, stat_own, stat_land,
    d_pre_out, d_pre_in, hidden_t, d_normed,
    partial, twin_part, landing, twin_part_b, landing_b, arrived, gain_parts, gain_land,
    whole_out, whole_mix, whole_in, land_out, land_mix, land_in, x_out, x_mix, x_in,
    sum_out, sum_mix, sum_in,
    send_sems, recv_sems, local_sems,
):
    place = Place()
    task = TaskPlace()
    wires = Wires(send_sems, recv_sems)
    me = place.me
    own_cols = pl.ds(pl.multiple_of(me * 256, 256), 256)
    first = load(own_tokens, tokens.at[pl.ds(0, 512), own_cols], local_sems, 0)
    g = gain[...]
    hi = g.astype(BF16).astype(F32)
    mid = (g - hi).astype(BF16).astype(F32)
    low = g - hi - mid
    row = sublanes((16, 256))
    rows = jnp.where(row == 0, hi, jnp.where(row == 1, mid, jnp.where(row == 2, low, 0.0)))
    tokens[pl.ds(512, 16), own_cols] = rows.astype(BF16)
    greet_everyone()
    first.wait()

    def token_view(block, half):
        rows = pl.ds(0, 256) if half == 0 else pl.ds(256, 272)
        return tokens.at[rows, pl.ds(pl.multiple_of(block * 256, 256), 256)]

    gather = Gather(place, wires, token_view)
    gather.open()
    get_in = load(w_in, w_in_v, local_sems, 1)
    get_mix = load(w_mix, w_mix_v, local_sems, 2)
    get_out = load(w_out, w_out_v, local_sems, 3)

    stat_own[...] = popart_rows(tasks, rewards, ends)
    statistics = AllPairs(wires, "task", 8, stat_land)
    for hop in range(1, 8):
        statistics.post(hop, lambda peer: stat_own)
    gather.middle()

    def slab(dz, opening=False):
        at = pl.multiple_of(plus(place.z, dz, 4) * 1024, 1024)

        def tile(m, carry):
            r = pl.ds(pl.multiple_of(m * 128, 128), 128)
            value = dot(tokens[r, pl.ds(at, 1024)], w_in_v[pl.ds(at, 1024), :])
            pre_in[r, :] = value if opening else pre_in[r, :] + value
            return carry

        lax.fori_loop(0, 4, tile, 0)

    get_in.wait()
    gather.wait_twin(gather.OWN, gather.ACROSS)
    slab(0, True)
    gather.late()
    gather.wait_twin(gather.FROM_UP, gather.UP_ACROSS)
    slab(1)
    gather.last()
    gather.wait_twin(gather.FROM_DOWN, gather.DOWN_ACROSS)
    slab(3)
    gather.wait_twin(gather.FAR, gather.FAR_ACROSS)
    slab(2)

    def activate(m, carry):
        r = pl.ds(pl.multiple_of(m * 128, 128), 128)
        v = pre_in[r, :]
        hidden_in[r, :] = (v * sigmoid(v)).astype(BF16)
        return carry

    lax.fori_loop(0, 4, activate, 0)
    get_mix.wait()
    scatter = Scatter(place, wires, partial, twin_part, landing)
    scatter.open(lambda half: wide_product(hidden_in, w_mix_v, partial, half, False))

    g3 = tokens[pl.ds(512, 16), :].astype(F32)
    gain_all[...] = g3[0:1, :] + g3[1:2, :] + g3[2:3, :]
    summed = stat_own[...]
    for hop in range(1, 8):
        statistics.wait(hop)
        summed = summed + stat_land[hop - 1]
    counts, totals, squares = summed[0:1, :], summed[1:2, :], summed[2:3, :]
    bias, pop_mean, pop_scale = vectors[0:1, :], vectors[1:2, :], vectors[2:3, :]
    mean, scale = popart_update(counts, totals, squares, pop_mean, pop_scale)
    is_value = lanes((1, 128)) >= ACTIONS
    ratio = jnp.where(is_value, pop_scale / scale, 1.0)
    new_bias = jnp.where(is_value, (pop_scale * bias + pop_mean - mean) / scale, bias)
    new_head[pl.ds(0, 75), :] = (head[...].astype(F32) * as_column(ratio)[0:75, :]).astype(BF16)
    new_head[pl.ds(75, 53), :] = jnp.zeros((53, 256), BF16)
    stats[...] = jnp.concatenate([mean, scale, new_bias, jnp.zeros((5, 128), F32)], axis=0)

    scatter.finish_far()
    scatter.finish_across()
    scatter.finish_near()
    first_env = me * 2
    columns = [
        step_columns(ref, first_env) for ref in (actions, rewards, ends, behaviour)
    ]
    columns[2] = DISCOUNT * (1.0 - columns[2])
    env = [
        jnp.sum(jnp.where(lanes((1, 32)) == first_env + e, tasks[...].astype(F32), 0.0), axis=1, keepdims=True)
        for e in (0, 1)
    ]
    game = jnp.where(sublanes((32, 128)) < 16, env[0], env[1])
    own_value = lanes((32, 128)) == game.astype(jnp.int32) + ACTIONS
    own_rows = pl.ds(pl.multiple_of(me * 32, 32), 32)

    def store(half, value):
        residual[:, half_cols(half)] = (
            value + tokens[own_rows, half_cols(half)].astype(F32)
        )

    scatter.finish(store)
    for m in range(2):
        v = residual[pl.ds(m * 16, 16), :]
        inverse = lax.rsqrt(jnp.mean(v * v, axis=1, keepdims=True) + NORM_EPS)
        normed[pl.ds(pl.multiple_of(me * 32 + m * 16, 16), 16), :] = (
            v * inverse * gain_all[...]
        ).astype(BF16)
    spread = Gather(place, wires, row_view(normed))
    spread.open()
    heads = AllPairs(wires, "tp", 16, head_land)

    def out_slab(dz):
        start = plus(place.z, dz, 4) * 128
        rows = pl.ds(pl.multiple_of(start, 128), 128)
        v = dot(normed[rows, :], w_out_v[...])
        pre_out[rows, :] = v
        hidden_out[rows, :] = (v * sigmoid(v)).astype(BF16)
        head_part[rows, :] = dot(hidden_out[rows, :], new_head[...], ((1,), (1,))).astype(BF16)

    spread.middle()
    get_out.wait()
    spread.wait_twin(spread.OWN, spread.ACROSS)
    out_slab(0)
    spread.late()
    spread.wait_twin(spread.FROM_UP, spread.UP_ACROSS)
    out_slab(1)
    spread.last()
    spread.wait_twin(spread.FROM_DOWN, spread.DOWN_ACROSS)
    out_slab(3)
    spread.wait_twin(spread.FAR, spread.FAR_ACROSS)
    out_slab(2)

    def frames_of(ref):
        return lambda device: ref.at[pl.ds(pl.multiple_of(device * 32, 32), 32), :]

    for hop in range(1, 16):
        heads.post(hop, frames_of(head_part))
    outputs = head_part[own_rows, :].astype(F32)
    for hop in range(1, 16):
        heads.wait(hop)
        outputs = outputs + head_land[hop - 1].astype(F32)
    d_own = loss_gradient(outputs + new_bias, own_value, columns, mean, scale)
    d_heads[own_rows, :] = d_own.astype(BF16)
    d_slot = wires.claim(15)
    d_view = frames_of(d_heads)
    for hop in range(1, 16):
        wires.send(d_view(me), d_view(me), d_slot + hop - 1, plus(me, hop, 16))
    wires.drain_all_but(15)
    for hop in range(1, 16):
        wires.arrived(d_view(plus(me, 16 - hop, 16)), d_slot + hop - 1)

    def pre_gradient(m, carry):
        r = pl.ds(pl.multiple_of(m * 128, 128), 128)
        d_hidden = dot(d_heads[r, :], new_head[...])
        d_pre_out[r, :] = (d_hidden * slope(pre_out[r, :])).astype(BF16)
        return carry

    lax.fori_loop(0, 4, pre_gradient, 0)
    scatter = Scatter(place, wires, partial, twin_part_b, landing_b)
    scatter.open(lambda half: wide_product(d_pre_out, w_out_v, partial, half, True))
    for_out = TaskSum(task, wires, slab_rows(512), whole_out, land_out, x_out, sum_out)
    for_mix = TaskSum(task, wires, slab_cols, whole_mix, land_mix, x_mix, sum_mix)
    for_in = TaskSum(task, wires, slab_rows(528), whole_in, land_in, x_in, sum_in)

    def tall_product(left, right, whole, height, dy):
        k = plus(task.y, dy, 4)

        def tile(n, carry):
            feature = pl.multiple_of(k * 1024 + n * 256, 256)
            at = pl.multiple_of((k * 2 + n // 2) * height + lax.rem(n, 2) * 256, 16)
            value = dot(left[pl.ds(0, 512), pl.ds(feature, 256)], right[...], ((0,), (0,)))
            whole[pl.ds(at, 256), :] = value.astype(BF16)
            return carry

        lax.fori_loop(0, 4, tile, 0)

    def mix_product(dy):
        k = plus(task.y, dy, 4)

        def tile(n, carry):
            at = pl.multiple_of(k * 1024 + n * 256, 256)
            whole_mix[:, pl.ds(at, 256)] = dot(hidden_t[...], arrived[:, pl.ds(at, 256)]).astype(BF16)
            return carry

        lax.fori_loop(0, 4, tile, 0)

    def out_product(dy):
        tall_product(normed, d_pre_out, whole_out, 512, dy)

    def in_product(dy):
        tall_product(tokens, d_pre_in, whole_in, 528, dy)

    out_product(2)
    for_out.far()
    scatter.finish_far()
    out_product(1)
    out_product(3)
    for_out.near()
    scatter.finish_across()
    out_product(0)
    scatter.finish_near()
    hidden_t[...] = hidden_in[...].T
    for_out.relay()

    def store(half, value):
        d_normed[:, half_cols(half)] = value

    scatter.finish(store)
    gain_rows = jnp.zeros((8, 4096), F32)
    for m in range(2):
        r = pl.ds(m * 16, 16)
        v = residual[r, :]
        inverse = lax.rsqrt(jnp.mean(v * v, axis=1, keepdims=True) + NORM_EPS)
        d = d_normed[r, :]
        scaled = d * gain_all[...]
        inner = jnp.sum(scaled * v, axis=1, keepdims=True)
        step = inverse * scaled - v * (inverse * inverse * inverse * inner * (1.0 / 4096))
        arrived[pl.ds(pl.multiple_of(me * 32 + m * 16, 16), 16), :] = step.astype(BF16)
        d_normed[r, :] = d * v * inverse
    gather = Gather(place, wires, row_view(arrived))
    gather.open()
    for m in range(4):
        gain_rows = gain_rows + d_normed[pl.ds(m * 8, 8), :]
    for n in range(16):
        gain_parts[n] = gain_rows[:, n * 256 : n * 256 + 256]
    for_out.fold()
    gains = AllPairs(wires, "tp", 16, gain_land)
    for hop in range(1, 16):
        gains.post(hop, lambda peer: gain_parts.at[peer])
    gather.middle()

    def hidden_slab(dz):
        rows = pl.ds(pl.multiple_of(plus(place.z, dz, 4) * 128, 128), 128)
        d = dot(arrived[rows, :], w_mix_v[...], ((1,), (1,)))
        d_pre_in[rows, :] = (d * slope(pre_in[rows, :])).astype(BF16)

    gather.wait_twin(gather.OWN, gather.ACROSS)
    hidden_slab(0)
    gather.late()
    for_out.finish()
    gather.wait_twin(gather.FROM_UP, gather.UP_ACROSS)
    hidden_slab(1)
    gather.last()
    gather.wait_twin(gather.FROM_DOWN, gather.DOWN_ACROSS)
    hidden_slab(3)
    gather.wait_twin(gather.FAR, gather.FAR_ACROSS)
    mix_product(2)
    for_mix.far()
    hidden_slab(2)
    mix_product(1)
    mix_product(3)
    for_mix.near()
    for_out.spread()
    mix_product(0)
    in_product(2)
    small = dot(d_heads[...], hidden_out[...], ((0,), (0,)))
    bias = jnp.sum(d_heads[...].astype(F32), axis=0, keepdims=True)
    gain_total = jnp.sum(gain_parts[me], axis=0, keepdims=True)
    for hop in range(1, 16):
        gains.wait(hop)
        gain_total = gain_total + jnp.sum(gain_land[hop - 1], axis=0, keepdims=True)
    row = lax.broadcasted_iota(jnp.int32, (128, 256), 0)
    bias = jnp.concatenate([bias, jnp.zeros((1, 128), F32)], axis=1)
    small = jnp.where(row == 80, bias, jnp.where(row == 88, gain_total, small)).astype(BF16)
    for n in range(8):
        whole_in[pl.ds(n * 528 + 512, 16), :] = small[n * 16 : n * 16 + 16, :]
    for_in.far()
    in_product(1)
    in_product(3)
    for_in.near()
    for_mix.relay()
    in_product(0)
    for_out.spread_far()
    for_in.relay()
    for_mix.fold()
    for_out.end()
    keep_out = load(sum_out, sum_out_hbm, local_sems, 4)
    for_in.fold()
    for_mix.finish()
    for_mix.spread()
    for_in.finish()
    for_mix.spread_far()
    for_in.spread()
    for_mix.end()
    keep_mix = load(sum_mix, sum_mix_hbm, local_sems, 5)
    for_in.spread_far()
    for_in.end()
    keep_in = load(sum_in, sum_in_hbm, local_sems, 6)
    wires.drain()
    for keep in (keep_out, keep_mix, keep_in):
        keep.wait()


def finish_kernel(
    sum_out, sum_mix, sum_in, new_head, stats,
    grad_in, grad_mix, grad_out, gain, head, bias, head_now, bias_now, mean, scale,
    out_b, mix_b, in_b, small_b, out_f, mix_f, in_f, sems,
):
    gets = []
    for n in range(8):
        r = pl.ds(n * 512, 512)
        gets.append(load(sum_in.at[pl.ds(n * 528, 512), :], in_b.at[r, :], sems, n))
    for n in range(8):
        gets.append(
            load(sum_in.at[pl.ds(n * 528 + 512, 16), :], small_b.at[pl.ds(n * 16, 16), :], sems, 8 + n)
        )
    for n in range(4):
        r = pl.ds(n * 64, 64)
        gets.append(load(sum_mix.at[r, :], mix_b.at[r, :], sems, 16 + n))
    for n in range(8):
        r = pl.ds(n * 512, 512)
        gets.append(load(sum_out.at[r, :], out_b.at[r, :], sems, 20 + n))
    puts = []
    for n in range(8):
        r = pl.ds(n * 512, 512)
        gets[n].wait()
        in_f[r, :] = in_b[r, :].astype(F32)
        puts.append(load(in_f.at[r, :], grad_in.at[r, :], sems, 28 + n))
    for n in range(4):
        r = pl.ds(n * 64, 64)
        gets[16 + n].wait()
        mix_f[r, :] = mix_b[r, :].astype(F32)
        puts.append(load(mix_f.at[r, :], grad_mix.at[r, :], sems, 36 + n))
    for n in range(8):
        r = pl.ds(n * 512, 512)
        gets[20 + n].wait()
        out_f[r, :] = out_b[r, :].astype(F32)
        puts.append(load(out_f.at[r, :], grad_out.at[r, :], sems, 40 + n))
    for n in range(8):
        gets[8 + n].wait()
    small = small_b[...].astype(F32)
    head[...] = small[0:75, :]
    bias[...] = small[80:81, 0:75]
    gain[...] = small[88:89, :]
    head_now[...] = new_head[0:75, :]
    values = pltpu.roll(stats[...], 128 - ACTIONS, 1)
    mean[...] = values[0:1, 0:TASKS]
    scale[...] = values[1:2, 0:TASKS]
    bias_now[...] = stats[2:3, 0:75]
    for put in puts:
        put.wait()


def hbm():
    return pl.BlockSpec(memory_space=pltpu.HBM)


def vmem():
    return pl.BlockSpec(memory_space=pltpu.VMEM)


def step_call(*arguments):
    v, h = vmem(), hbm()
    scratch = [
        ((528, 4096), BF16), ((4096, 256), BF16), ((256, 4096), BF16), ((4096, 256), BF16),
        ((512, 256), F32), ((512, 256), BF16), ((32, 4096), F32), ((1, 4096), F32),
        ((512, 4096), BF16),
        ((512, 256), F32), ((512, 256), BF16), ((512, 128), BF16), ((15, 32, 128), BF16),
        ((512, 128), BF16), ((8, 128), F32), ((7, 8, 128), F32),
        ((512, 256), BF16), ((512, 256), BF16), ((256, 512), BF16), ((32, 4096), F32),
        ((512, 4096), BF16), ((8, 32, 4096), BF16), ((7, 32, 4096), BF16),
        ((8, 32, 4096), BF16), ((7, 32, 4096), BF16), ((512, 4096), BF16),
        ((16, 8, 256), F32), ((15, 8, 256), F32),
        ((4096, 256), BF16), ((256, 4096), BF16), ((4224, 256), BF16),
        ((3, 2, 512, 256), BF16), ((3, 2, 256, 512), BF16), ((3, 2, 528, 256), BF16),
        ((512, 256), BF16), ((256, 512), BF16), ((528, 256), BF16),
        ((4096, 256), BF16), ((256, 4096), BF16), ((4224, 256), BF16),
    ]
    return pl.pallas_call(
        step_kernel,
        out_shape=[
            jax.ShapeDtypeStruct((4096, 256), BF16),
            jax.ShapeDtypeStruct((256, 4096), BF16),
            jax.ShapeDtypeStruct((4224, 256), BF16),
            jax.ShapeDtypeStruct((128, 256), BF16),
            jax.ShapeDtypeStruct((8, 128), F32),
        ],
        in_specs=[h, v, h, h, h, v, v, v, v, v, v, v],
        out_specs=[h, h, h, v, v],
        scratch_shapes=[pltpu.VMEM(*s) for s in scratch]
        + [pltpu.SemaphoreType.DMA((SENDS,)), pltpu.SemaphoreType.DMA((RECEIVES,)), pltpu.SemaphoreType.DMA((7,))],
        compiler_params=pltpu.CompilerParams(
            collective_id=0, has_side_effects=True, vmem_limit_bytes=63 * 2**20
        ),
        name="step",
    )(*arguments)


def finish_call(*arguments):
    v, h = vmem(), hbm()
    return pl.pallas_call(
        finish_kernel,
        out_shape=[
            jax.ShapeDtypeStruct((4096, 256), F32),
            jax.ShapeDtypeStruct((256, 4096), F32),
            jax.ShapeDtypeStruct((4096, 256), F32),
            jax.ShapeDtypeStruct((1, 256), F32),
            jax.ShapeDtypeStruct((75, 256), F32),
            jax.ShapeDtypeStruct((1, 75), F32),
            jax.ShapeDtypeStruct((75, 256), BF16),
            jax.ShapeDtypeStruct((1, 75), F32),
            jax.ShapeDtypeStruct((1, TASKS), F32),
            jax.ShapeDtypeStruct((1, TASKS), F32),
        ],
        in_specs=[h, h, h, v, v],
        out_specs=[h, h, h, v, v, v, v, v, v, v],
        scratch_shapes=[
            pltpu.VMEM((4096, 256), BF16),
            pltpu.VMEM((256, 4096), BF16),
            pltpu.VMEM((4096, 256), BF16),
            pltpu.VMEM((128, 256), BF16),
            pltpu.VMEM((4096, 256), F32),
            pltpu.VMEM((256, 4096), F32),
            pltpu.VMEM((4096, 256), F32),
            pltpu.SemaphoreType.DMA((48,)),
        ],
        compiler_params=pltpu.CompilerParams(vmem_limit_bytes=48 * 2**20),
        name="finish",
    )(*arguments)


def on_device(
    observations, gain, w_in, w_mix, w_out, w_head, head_bias, pop_mean, pop_scale,
    task_indices, actions, rewards, episode_ends, behaviour_log_prob,
):
    pad = (ACTIONS, 128 - ACTIONS - TASKS)
    vectors = jnp.stack(
        [
            jnp.pad(head_bias, (0, 128 - ACTIONS - TASKS)),
            jnp.pad(pop_mean, pad),
            jnp.pad(pop_scale, pad, constant_values=1.0),
        ]
    )
    sums = step_call(
        observations.reshape(512, 256),
        gain.reshape(1, 256),
        w_in,
        w_mix,
        w_out,
        w_head.T,
        vectors,
        task_indices.reshape(1, 32),
        actions.T,
        rewards.T,
        episode_ends.T,
        behaviour_log_prob.T,
    )
    (
        grad_in, grad_mix, grad_out, grad_gain, grad_head, grad_bias,
        new_head, new_bias, mean, scale,
    ) = finish_call(*sums)
    return (
        grad_in,
        grad_mix,
        grad_out,
        grad_gain.reshape(256),
        grad_head.T,
        grad_bias.reshape(75),
        new_head.T,
        new_bias.reshape(75),
        mean.reshape(TASKS),
        scale.reshape(TASKS),
    )


def solution(mesh):
    in_specs = (
        P("task", None, "tp"),
        P("tp"),
        P(None, "tp"),
        P("tp", None),
        P(None, "tp"),
        P("tp", None),
        P(),
        P(),
        P(),
        P("task"),
        P("task", None),
        P("task", None),
        P("task", None),
        P("task", None),
    )
    out_specs = (
        P(None, "tp"),
        P("tp", None),
        P(None, "tp"),
        P("tp"),
        P("tp", None),
        P(),
        P("tp", None),
        P(),
        P(),
        P(),
    )
    return jax.shard_map(
        on_device, mesh=mesh, in_specs=in_specs, out_specs=out_specs, check_vma=False
    )
```

time: 289 us -> 239 us (0.83)
  other arithmetic: 20.4 us -> 0.59 us
  starting transfers between devices: 15.4 us -> 0 us
  waiting for transfers between devices: 10.9 us -> 0 us
  Pallas kernels: 219 us -> 229 us
  matrix products: 7.08 us -> 0 us
  local copies, waits for them, and re-layouts: 12.9 us -> 6.1 us
    all_to_all x3 -> x0, starting transfers between devices: 15.4 us -> none  [the longest x2 11.4 us: sent_to_all(): return lax.all_to_all(copies, axis, split_axis=0, concat_axis=0, tiled=True)]
    add x32 -> x0, other arithmetic: 10.9 us -> none  [the longest x30 10.9 us: advance(): latest = column[0] + column[1] * running]
    all_to_all x3 -> x0, waiting for transfers between devices: 10.9 us -> none  [the longest x1 6.03 us: sum_at_owner(): lax.all_to_all(parts, axis, split_axis=0, concat_axis=0, tiled=True)]
    pallas_call x2, Pallas kernels: 219 us -> 229 us  [the longest x1 223 us: step_call(): pl.pallas_call(step_kernel, out_shape=[jax.ShapeDtypeStruct((4096, 256),...]
    dot_general x6 -> x0, matrix products: 7.08 us -> none  [the longest x1 4.93 us: on_device(): pre_out = jnp.dot(normed_all, w_out, preferred_element_type=jnp.float32)]
    convert_element_type x5 -> x0, other arithmetic: 5.02 us -> none  [the longest x1 2.5 us: on_device(): sum_mix.astype(jnp.float32)]
    slice x5 -> x0, local copies, waits for them, and re-layouts: 3.29 us -> none  [the longest x1 1.73 us: on_device(): sum_in[:, :512].astype(jnp.float32).reshape(full_width, part_width)]
  transfers between devices with their start and end apart: 3 -> 0, of which waited for: 2 -> 0; matrix products, arithmetic and copies ran while one was open for 3% -> 0% of each run, Pallas kernels for 25% -> 0%
where the time goes in v2:
time: 239 us; the launch traced here: 237 us
  Pallas kernels  229 us (96%)
  local copies, waits for them, and re-layouts  6.1 us (3%)
    pallas_call x1, Pallas kernels, step_call(): pl.pallas_call(step_kernel, out_shape=[jax.ShapeDtypeStruct((4096, 256),...  223 us
    pallas_call x1, Pallas kernels, finish_call(): pl.pallas_call(finish_kernel, out_shape=[jax.ShapeDtypeStruct((4096, 256)...  6.59 us

profile of v2, /device:TPU:1, one launch (start us, length us, event | category | flops | bytes accessed | tf_op | source)
XLA Modules:
  0.0 236.8 jit_solution(10865851307652367521)
XLA Ops:
  0.6 0.7 pad_bitcast_fusion.2
  1.3 0.7 pad_bitcast_fusion
  2.0 0.6 pad_maximum_fusion.vectors
  2.6 222.7 %step.1 = (bf16[4096,256]{1,0:T(8,128)(2,1)}, bf16[256,4096]{1,0:T(8,128)(2,1)}, bf16[4224,256]{1,0:T(8,128)(2,1)}, bf16[128,256]{1,0:T(8,128)(2,1)}, f32[8,128]{1,0:T(8,128)}) custom-call(bf16[512,256]{1,0:T(8,128)(2,1)} %bitcast.21, f32[1,256]{1,0:T(1,128)} %bitcast.27, bf16[4096,256]{1,0:T(8,128)(2,1)} %w_in.1, bf16[256,4096]{1,0:T(8,128)(2,1)} %w_mix.1, ...), custom_call_target="tpu_custom_call" | custom-call | tf_op jit(solution)/shard_map/step/pallas_call | solution.py:947
  225.4 0.0 copy-start
  225.4 1.6 copy-done
  227.0 0.0 copy-start.1
  227.0 1.6 copy-done.1
  228.6 0.0 copy-start.2
  228.6 0.8 copy-done.2
  229.4 0.0 copy-start.3
  229.4 0.7 copy-done.3
  230.1 6.6 %finish.1 = (f32[4096,256]{1,0:T(8,128)}, f32[256,4096]{1,0:T(8,128)}, f32[4096,256]{1,0:T(8,128)}, f32[1,256]{1,0:T(1,128)}, f32[75,256]{1,0:T(8,128)}, /*index...) custom-call(bf16[4096,256]{1,0:T(8,128)(2,1)S(1)} %copy-done, ...), custom_call_target="tpu_custom_call" | custom-call | tf_op jit(solution)/shard_map/finish/pallas_call | solution.py:969
Async XLA Ops:
  225.4 1.6 copy-start
  227.0 1.6 copy-start.1
  228.6 0.8 copy-start.2
  229.4 0.7 copy-start.3

commit v3 on v2

--- a/solution.py
+++ b/solution.py
@@ -13,8 +13,8 @@
 POPART_PRIOR = 64.0
 NORM_EPS = 1e-06
 LOSS_WEIGHT = 256**-0.5
-SENDS = 248
-RECEIVES = 248
+SENDS = 148
+RECEIVES = 208
 
 
 MESH = pl.DeviceIdType.MESH
@@ -47,7 +47,6 @@
         self.send_sems = send_sems
         self.recv_sems = recv_sems
         self.sent = []
-        self.drained = 0
         self.slots = 0
 
     def claim(self, count):
@@ -77,24 +76,20 @@
             device_id_type=MESH,
         ).wait_recv()
 
-    def drain_all_but(self, last):
-        for copy in self.sent[: len(self.sent) - last]:
+    def drain(self):
+        for copy in self.sent:
             copy.wait_send()
-        self.drained = len(self.sent) - last
-
-    def drain(self):
-        for copy in self.sent[self.drained :]:
-            copy.wait_send()
+        self.sent = []
 
 
 class Gather:
     ACROSS, FROM_DOWN, FROM_UP, DOWN_ACROSS, UP_ACROSS, FAR, FAR_ACROSS, OWN = range(8)
 
-    def __init__(self, place, wires, view):
+    def __init__(self, place, wires, view, first):
         self.place = place
         self.wires = wires
         self.view = view
-        self.first = wires.claim(30)
+        self.first = first
         p = place
         self.block = {
             self.ACROSS: p.at(0, 1),
@@ -141,6 +136,11 @@
             self.to_twin(self.OWN, half)
 
     def middle(self):
+        self.middle_near()
+        self.middle_across()
+        self.middle_far()
+
+    def middle_near(self):
         p = self.place
         self.wait(self.FROM_DOWN, 0)
         self.pass_on(self.FROM_DOWN, 0, p.up, self.FAR)
@@ -154,15 +154,20 @@
         self.pass_on(self.ACROSS, 0, p.up, self.DOWN_ACROSS)
         self.to_twin(self.ACROSS, 0)
         self.to_twin(self.FROM_UP, 1)
+
+    def middle_across(self):
+        p = self.place
         self.wait(self.FROM_DOWN, 1)
         self.to_twin(self.FROM_DOWN, 1)
         self.wait(self.ACROSS, 1)
         self.pass_on(self.ACROSS, 1, p.up, self.DOWN_ACROSS)
         self.pass_on(self.ACROSS, 1, p.down, self.UP_ACROSS)
         self.to_twin(self.ACROSS, 1)
+
+    def middle_far(self):
         for half in HALVES:
             self.wait(self.FAR, half)
-            self.pass_on(self.FAR, half, p.across, self.FAR_ACROSS)
+            self.pass_on(self.FAR, half, self.place.across, self.FAR_ACROSS)
             self.to_twin(self.FAR, half)
 
     def late(self):
@@ -185,13 +190,13 @@
     G, D, E, F, A, B, C = range(7)
     ORDER = ((2, 1), (1, 1), (3, 1), (1, 0), (3, 0), (2, 0), (0, 1), (0, 0))
 
-    def __init__(self, place, wires, partial, twin_part, landing):
+    def __init__(self, place, wires, partial, twin_part, landing, first):
         self.place = place
         self.wires = wires
         self.partial = partial
         self.twin_part = twin_part
         self.landing = landing
-        self.first = wires.claim(30)
+        self.first = first
 
     def rows(self, where, dc=0):
         return pl.ds(pl.multiple_of(self.place.at(*where, dc) * 32, 32), 32)
@@ -349,6 +354,8 @@
             self.post(own, self.land.at[kind, part], slot, peer)
 
     def local(self, part):
+        if self.land is None:
+            return self.view(self.whole, part)[...].astype(F32)
         return (
             self.slab(self.whole, 0, part)[...].astype(F32)
             + self.land[self.B, part].astype(F32)
@@ -356,6 +363,10 @@
         )
 
     def fold(self):
+        if self.land is None:
+            away = self.view(self.whole, 1 - self.place.xh)
+            self.post(away, self.land_x, 6, self.place.across)
+            return
         for kind, part, slot in ((self.B, 1, 3), (self.C, 0, 4), (self.B, 0, 2), (self.C, 1, 5)):
             self.wait(self.land.at[kind, part], slot)
         other = 1 - self.place.xh
@@ -413,6 +424,64 @@
     def end(self):
         self.get(self.FAR)
         self.get(self.FAR_ACROSS)
+
+
+class RingGather:
+    FROM_DOWN, FROM_UP, FAR = range(3)
+
+    def __init__(self, place, wires, view):
+        self.place = place
+        self.wires = wires
+        self.view = view
+        self.first = wires.claim(6)
+
+    def block(self, kind, half):
+        dy = {self.FROM_DOWN: 3, self.FROM_UP: 1, self.FAR: 2}[kind]
+        return self.view(plus(self.place.y, dy, 4), half)
+
+    def post(self, v, kind, half, peer):
+        self.wires.send(v, v, self.first + kind * 2 + half, peer, "task")
+
+    def wait(self, kind, half):
+        self.wires.arrived(self.block(kind, half), self.first + kind * 2 + half, "task")
+
+    def open(self):
+        p = self.place
+        for up_half, down_half in ((0, 1), (1, 0)):
+            self.post(self.view(p.y, up_half), self.FROM_DOWN, up_half, p.up)
+            self.post(self.view(p.y, down_half), self.FROM_UP, down_half, p.down)
+
+    def relay(self):
+        self.wait(self.FROM_DOWN, 0)
+        self.post(self.block(self.FROM_DOWN, 0), self.FAR, 0, self.place.up)
+        self.wait(self.FROM_UP, 1)
+        self.post(self.block(self.FROM_UP, 1), self.FAR, 1, self.place.down)
+
+    def end(self):
+        self.wait(self.FROM_DOWN, 1)
+        self.wait(self.FROM_UP, 0)
+        self.wait(self.FAR, 0)
+        self.wait(self.FAR, 1)
+
+
+class RingExchange:
+    def __init__(self, place, wires, source, land):
+        self.place = place
+        self.wires = wires
+        self.source = source
+        self.land = land
+        self.first = wires.claim(3)
+
+    def open(self):
+        p = self.place
+        for dy in (2, 1, 3):
+            y = plus(p.y, dy, 4)
+            self.wires.send(
+                self.source(y), self.land(4 - dy), self.first + 3 - dy, p.xh * 4 + y, "task"
+            )
+
+    def wait(self, dy):
+        self.wires.arrived(self.land(dy), self.first + dy - 1, "task")
 
 
 def slope(v):
@@ -568,14 +637,16 @@
     tokens, w_in_v, w_mix_v, w_out_v, pre_in, hidden_in, residual, gain_all, normed,
     pre_out, hidden_out, head_part, head_land, d_heads, stat_own, stat_land,
     d_pre_out, d_pre_in, hidden_t, d_normed,
+    hidden_ring, far_tokens, residual_ring, small_own, small_land,
     partial, twin_part, landing, twin_part_b, landing_b, arrived, gain_parts, gain_land,
-    whole_out, whole_mix, whole_in, land_out, land_mix, land_in, x_out, x_mix, x_in,
+    whole_out, whole_mix, whole_in, land_out, x_out, x_mix, x_in,
     sum_out, sum_mix, sum_in,
     send_sems, recv_sems, local_sems,
 ):
     place = Place()
     task = TaskPlace()
     wires = Wires(send_sems, recv_sems)
+    gather_a, gather_b, scatter_slots = wires.claim(30), wires.claim(30), wires.claim(30)
     me = place.me
     own_cols = pl.ds(pl.multiple_of(me * 256, 256), 256)
     first = load(own_tokens, tokens.at[pl.ds(0, 512), own_cols], local_sems, 0)
@@ -593,7 +664,7 @@
         rows = pl.ds(0, 256) if half == 0 else pl.ds(256, 272)
         return tokens.at[rows, pl.ds(pl.multiple_of(block * 256, 256), 256)]
 
-    gather = Gather(place, wires, token_view)
+    gather = Gather(place, wires, token_view, gather_a)
     gather.open()
     get_in = load(w_in, w_in_v, local_sems, 1)
     get_mix = load(w_mix, w_mix_v, local_sems, 2)
@@ -631,14 +702,30 @@
     def activate(m, carry):
         r = pl.ds(pl.multiple_of(m * 128, 128), 128)
         v = pre_in[r, :]
-        hidden_in[r, :] = (v * sigmoid(v)).astype(BF16)
+        hidden = (v * sigmoid(v)).astype(BF16)
+        hidden_in[r, :] = hidden
+        hidden_ring[pl.ds(m * 4, 4), task.y] = hidden.reshape(4, 32, 256)
         return carry
 
     lax.fori_loop(0, 4, activate, 0)
     get_mix.wait()
-    scatter = Scatter(place, wires, partial, twin_part, landing)
+    scatter = Scatter(place, wires, partial, twin_part, landing, scatter_slots)
     scatter.open(lambda half: wide_product(hidden_in, w_mix_v, partial, half, False))
 
+    for_hidden = RingGather(
+        task, wires, lambda y, half: hidden_ring.at[pl.ds(half * 8, 8), y]
+    )
+    for_hidden.open()
+    core_rows = pl.ds(pl.multiple_of(place.c * 256, 256), 256)
+    twin_rows = pl.ds(pl.multiple_of(256 - place.c * 256, 256), 256)
+    for_tokens = RingExchange(
+        task,
+        wires,
+        lambda y: tokens.at[core_rows, pl.ds(pl.multiple_of(y * 1024, 1024), 1024)],
+        lambda dy: far_tokens.at[dy - 1, core_rows, :],
+    )
+    for_tokens.open()
+    token_slot = wires.claim(3)
     g3 = tokens[pl.ds(512, 16), :].astype(F32)
     gain_all[...] = g3[0:1, :] + g3[1:2, :] + g3[2:3, :]
     summed = stat_own[...]
@@ -683,8 +770,9 @@
         normed[pl.ds(pl.multiple_of(me * 32 + m * 16, 16), 16), :] = (
             v * inverse * gain_all[...]
         ).astype(BF16)
-    spread = Gather(place, wires, row_view(normed))
+    spread = Gather(place, wires, row_view(normed), gather_b)
     spread.open()
+    for_hidden.relay()
     heads = AllPairs(wires, "tp", 16, head_land)
 
     def out_slab(dz):
@@ -713,6 +801,15 @@
 
     for hop in range(1, 16):
         heads.post(hop, frames_of(head_part))
+    for dy in (1, 2, 3):
+        for_tokens.wait(dy)
+        share = far_tokens.at[dy - 1, core_rows, :]
+        wires.send(share, share, token_slot + dy - 1, place.partner)
+    for_hidden.end()
+    for b in range(4):
+        hidden_t[:, b * 512 : b * 512 + 512] = (
+            hidden_ring[b * 4 : b * 4 + 4].reshape(512, 256).T
+        )
     outputs = head_part[own_rows, :].astype(F32)
     for hop in range(1, 16):
         heads.wait(hop)
@@ -723,9 +820,9 @@
     d_view = frames_of(d_heads)
     for hop in range(1, 16):
         wires.send(d_view(me), d_view(me), d_slot + hop - 1, plus(me, hop, 16))
-    wires.drain_all_but(15)
     for hop in range(1, 16):
         wires.arrived(d_view(plus(me, 16 - hop, 16)), d_slot + hop - 1)
+    wires.drain()
 
     def pre_gradient(m, carry):
         r = pl.ds(pl.multiple_of(m * 128, 128), 128)
@@ -734,11 +831,11 @@
         return carry
 
     lax.fori_loop(0, 4, pre_gradient, 0)
-    scatter = Scatter(place, wires, partial, twin_part_b, landing_b)
+    scatter = Scatter(place, wires, partial, twin_part_b, landing_b, scatter_slots)
     scatter.open(lambda half: wide_product(d_pre_out, w_out_v, partial, half, True))
     for_out = TaskSum(task, wires, slab_rows(512), whole_out, land_out, x_out, sum_out)
-    for_mix = TaskSum(task, wires, slab_cols, whole_mix, land_mix, x_mix, sum_mix)
-    for_in = TaskSum(task, wires, slab_rows(528), whole_in, land_in, x_in, sum_in)
+    for_mix = TaskSum(task, wires, slab_cols, whole_mix, None, x_mix, sum_mix)
+    for_in = TaskSum(task, wires, slab_rows(528), whole_in, None, x_in, sum_in)
 
     def tall_product(left, right, whole, height, dy):
         k = plus(task.y, dy, 4)
@@ -752,21 +849,34 @@
 
         lax.fori_loop(0, 4, tile, 0)
 
-    def mix_product(dy):
-        k = plus(task.y, dy, 4)
-
+    def mix_product(part):
         def tile(n, carry):
-            at = pl.multiple_of(k * 1024 + n * 256, 256)
-            whole_mix[:, pl.ds(at, 256)] = dot(hidden_t[...], arrived[:, pl.ds(at, 256)]).astype(BF16)
+            at = pl.multiple_of(part * 512 + n * 256, 256)
+            whole_mix[:, pl.ds(at, 256)] = dot(
+                hidden_t[...], residual_ring[:, pl.ds(at, 256)]
+            ).astype(BF16)
             return carry
 
-        lax.fori_loop(0, 4, tile, 0)
+        lax.fori_loop(0, 2, tile, 0)
+
+    def in_product(part):
+        def tile(n, carry):
+            at = pl.multiple_of(part * 512 + n * 256, 256)
+            here = pl.ds(pl.multiple_of(task.y * 1024 + at, 256), 256)
+            value = dot(tokens[pl.ds(0, 512), here], d_pre_in[task.y], ((0,), (0,)))
+            for dy in (1, 2, 3):
+                value = value + dot(
+                    far_tokens[dy - 1, :, pl.ds(at, 256)],
+                    d_pre_in[plus(task.y, dy, 4)],
+                    ((0,), (0,)),
+                )
+            whole_in[pl.ds(pl.multiple_of(part * 528 + n * 256, 16), 256), :] = value.astype(BF16)
+            return carry
+
+        lax.fori_loop(0, 2, tile, 0)
 
     def out_product(dy):
         tall_product(normed, d_pre_out, whole_out, 512, dy)
-
-    def in_product(dy):
-        tall_product(tokens, d_pre_in, whole_in, 528, dy)
 
     out_product(2)
     for_out.far()
@@ -776,9 +886,8 @@
     for_out.near()
     scatter.finish_across()
     out_product(0)
+    for_out.relay()
     scatter.finish_near()
-    hidden_t[...] = hidden_in[...].T
-    for_out.relay()
 
     def store(half, value):
         d_normed[:, half_cols(half)] = value
@@ -795,26 +904,58 @@
         step = inverse * scaled - v * (inverse * inverse * inverse * inner * (1.0 / 4096))
         arrived[pl.ds(pl.multiple_of(me * 32 + m * 16, 16), 16), :] = step.astype(BF16)
         d_normed[r, :] = d * v * inverse
-    gather = Gather(place, wires, row_view(arrived))
+    gather = Gather(place, wires, row_view(arrived), gather_a)
     gather.open()
+    ring_rows = lambda y: pl.ds(pl.multiple_of(me * 128 + y * 32, 32), 32)
+    quarter = lambda y: pl.ds(pl.multiple_of(y * 1024, 1024), 1024)
+    own32 = pl.ds(pl.multiple_of(me * 32, 32), 32)
+    residual_ring[ring_rows(task.y), :] = arrived[own32, quarter(task.y)]
+    for_residual = RingExchange(
+        task,
+        wires,
+        lambda y: arrived.at[own32, quarter(y)],
+        lambda dy: residual_ring.at[ring_rows(plus(task.y, dy, 4)), :],
+    )
+    for dy in (2, 1, 3):
+        y = plus(task.y, dy, 4)
+        wires.send(
+            arrived.at[own32, quarter(y)],
+            residual_ring.at[ring_rows(task.y), :],
+            for_residual.first + 3 - dy,
+            task.xh * 4 + y,
+            "task",
+        )
     for m in range(4):
         gain_rows = gain_rows + d_normed[pl.ds(m * 8, 8), :]
     for n in range(16):
         gain_parts[n] = gain_rows[:, n * 256 : n * 256 + 256]
-    for_out.fold()
     gains = AllPairs(wires, "tp", 16, gain_land)
     for hop in range(1, 16):
         gains.post(hop, lambda peer: gain_parts.at[peer])
-    gather.middle()
 
     def hidden_slab(dz):
         rows = pl.ds(pl.multiple_of(plus(place.z, dz, 4) * 128, 128), 128)
         d = dot(arrived[rows, :], w_mix_v[...], ((1,), (1,)))
-        d_pre_in[rows, :] = (d * slope(pre_in[rows, :])).astype(BF16)
-
+        d_pre_in[task.y, rows, :] = (d * slope(pre_in[rows, :])).astype(BF16)
+
+    gather.middle_near()
+    for_out.fold()
+    gather.middle_across()
+    gather.middle_far()
     gather.wait_twin(gather.OWN, gather.ACROSS)
     hidden_slab(0)
     gather.late()
+    for dy in (1, 3, 2):
+        for_residual.wait(dy)
+    ring = Gather(
+        place,
+        wires,
+        lambda block, half: residual_ring.at[
+            pl.ds(pl.multiple_of(block * 128, 128), 128), pl.ds(half * 512, 512)
+        ],
+        gather_b,
+    )
+    ring.open()
     for_out.finish()
     gather.wait_twin(gather.FROM_UP, gather.UP_ACROSS)
     hidden_slab(1)
@@ -822,48 +963,63 @@
     gather.wait_twin(gather.FROM_DOWN, gather.DOWN_ACROSS)
     hidden_slab(3)
     gather.wait_twin(gather.FAR, gather.FAR_ACROSS)
-    mix_product(2)
-    for_mix.far()
     hidden_slab(2)
-    mix_product(1)
-    mix_product(3)
-    for_mix.near()
-    for_out.spread()
-    mix_product(0)
-    in_product(2)
+    for_slope = RingGather(
+        task,
+        wires,
+        lambda y, half: d_pre_in.at[y, pl.ds(half * 256, 256), :],
+    )
+    for_slope.open()
     small = dot(d_heads[...], hidden_out[...], ((0,), (0,)))
     bias = jnp.sum(d_heads[...].astype(F32), axis=0, keepdims=True)
     gain_total = jnp.sum(gain_parts[me], axis=0, keepdims=True)
     for hop in range(1, 16):
         gains.wait(hop)
         gain_total = gain_total + jnp.sum(gain_land[hop - 1], axis=0, keepdims=True)
-    row = lax.broadcasted_iota(jnp.int32, (128, 256), 0)
+    row = sublanes((128, 256))
     bias = jnp.concatenate([bias, jnp.zeros((1, 128), F32)], axis=1)
-    small = jnp.where(row == 80, bias, jnp.where(row == 88, gain_total, small)).astype(BF16)
-    for n in range(8):
-        whole_in[pl.ds(n * 528 + 512, 16), :] = small[n * 16 : n * 16 + 16, :]
-    for_in.far()
-    in_product(1)
-    in_product(3)
-    for_in.near()
-    for_mix.relay()
-    in_product(0)
+    small_own[...] = jnp.where(
+        row == 80, bias, jnp.where(row == 88, gain_total, small)
+    ).astype(BF16)
+    small_rows = lambda y: small_own.at[pl.ds(pl.multiple_of(y * 32, 32), 32), :]
+    for_small = RingExchange(task, wires, small_rows, lambda dy: small_land.at[dy - 1])
+    for_small.open()
+    ring.middle_near()
+    for_out.spread()
+    ring.middle_across()
+    for_slope.relay()
+    ring.middle_far()
+    ring.late()
+    for dy in (1, 2, 3):
+        wires.arrived(far_tokens.at[dy - 1, twin_rows, :], token_slot + dy - 1)
+    extra = small_rows(task.y)[...].astype(F32)
+    for dy in (1, 3, 2):
+        for_small.wait(dy)
+        extra = extra + small_land[dy - 1].astype(F32)
+    for part in (0, 1):
+        whole_in[pl.ds(part * 528 + 512, 16), :] = extra[part * 16 : part * 16 + 16, :].astype(BF16)
+    for_slope.end()
+    in_product(1 - task.xh)
+    for_in.fold()
+    ring.last()
+    in_product(task.xh)
+    ring.wait_twin(*range(8))
+    mix_product(1 - task.xh)
+    for_mix.fold()
+    mix_product(task.xh)
     for_out.spread_far()
-    for_in.relay()
-    for_mix.fold()
+    for_in.finish()
+    for_in.spread()
+    for_mix.finish()
+    for_in.spread_far()
     for_out.end()
     keep_out = load(sum_out, sum_out_hbm, local_sems, 4)
-    for_in.fold()
-    for_mix.finish()
     for_mix.spread()
-    for_in.finish()
+    for_in.end()
+    keep_in = load(sum_in, sum_in_hbm, local_sems, 6)
     for_mix.spread_far()
-    for_in.spread()
     for_mix.end()
     keep_mix = load(sum_mix, sum_mix_hbm, local_sems, 5)
-    for_in.spread_far()
-    for_in.end()
-    keep_in = load(sum_in, sum_in_hbm, local_sems, 6)
     wires.drain()
     for keep in (keep_out, keep_mix, keep_in):
         keep.wait()
@@ -935,12 +1091,14 @@
         ((512, 4096), BF16),
         ((512, 256), F32), ((512, 256), BF16), ((512, 128), BF16), ((15, 32, 128), BF16),
         ((512, 128), BF16), ((8, 128), F32), ((7, 8, 128), F32),
-        ((512, 256), BF16), ((512, 256), BF16), ((256, 512), BF16), ((32, 4096), F32),
+        ((512, 256), BF16), ((4, 512, 256), BF16), ((256, 2048), BF16), ((32, 4096), F32),
+        ((16, 4, 32, 256), BF16), ((3, 512, 1024), BF16), ((2048, 1024), BF16),
+        ((128, 256), BF16), ((3, 32, 256), BF16),
         ((512, 4096), BF16), ((8, 32, 4096), BF16), ((7, 32, 4096), BF16),
         ((8, 32, 4096), BF16), ((7, 32, 4096), BF16), ((512, 4096), BF16),
         ((16, 8, 256), F32), ((15, 8, 256), F32),
-        ((4096, 256), BF16), ((256, 4096), BF16), ((4224, 256), BF16),
-        ((3, 2, 512, 256), BF16), ((3, 2, 256, 512), BF16), ((3, 2, 528, 256), BF16),
+        ((4096, 256), BF16), ((256, 1024), BF16), ((1056, 256), BF16),
+        ((3, 2, 512, 256), BF16),
         ((512, 256), BF16), ((256, 512), BF16), ((528, 256), BF16),
         ((4096, 256), BF16), ((256, 4096), BF16), ((4224, 256), BF16),
     ]
@@ -992,7 +1150,7 @@
             pltpu.VMEM((4096, 256), F32),
             pltpu.SemaphoreType.DMA((48,)),
         ],
-        compiler_params=pltpu.CompilerParams(vmem_limit_bytes=48 * 2**20),
+        compiler_params=pltpu.CompilerParams(vmem_limit_bytes=63 * 2**20),
         name="finish",
     )(*arguments)
 

time: 239 us -> 218 us (0.912)
  Pallas kernels: 229 us -> 213 us
  local copies, waits for them, and re-layouts: 6.1 us -> 1.4 us
    pallas_call x1, Pallas kernels: 223 us -> 205 us  [step_call(): pl.pallas_call(step_kernel, out_shape=[jax.ShapeDtypeStruct((4096, 256),...]
    unnamed x8 -> x0, local copies, waits for them, and re-layouts: 4.69 us -> none
where the time goes in v3:
time: 218 us; the launch traced here: 215 us
  Pallas kernels  213 us (98%)
    pallas_call x1, Pallas kernels, step_call(): pl.pallas_call(step_kernel, out_shape=[jax.ShapeDtypeStruct((4096, 256),...  205 us
    pallas_call x1, Pallas kernels, finish_call(): pl.pallas_call(finish_kernel, out_shape=[jax.ShapeDtypeStruct((4096, 256)...  7.93 us

profile of v3, /device:TPU:1, one launch (start us, length us, event | category | flops | bytes accessed | tf_op | source)
XLA Modules:
  0.0 215.4 jit_solution(17015706153584398393)
XLA Ops:
  0.6 0.7 pad_bitcast_fusion.2
  1.3 0.7 pad_bitcast_fusion
  2.0 0.6 pad_maximum_fusion.vectors
  2.6 204.7 %step.1 = (bf16[4096,256]{1,0:T(8,128)(2,1)}, bf16[256,4096]{1,0:T(8,128)(2,1)}, bf16[4224,256]{1,0:T(8,128)(2,1)}, bf16[128,256]{1,0:T(8,128)(2,1)}, f32[8,128]{1,0:T(8,128)}) custom-call(bf16[512,256]{1,0:T(8,128)(2,1)} %bitcast.21, f32[1,256]{1,0:T(1,128)} %bitcast.27, bf16[4096,256]{1,0:T(8,128)(2,1)} %w_in.1, bf16[256,4096]{1,0:T(8,128)(2,1)} %w_mix.1, ...), custom_call_target="tpu_custom_call" | custom-call | tf_op jit(solution)/shard_map/step/pallas_call | solution.py:1105
  207.3 7.9 %finish.1 = (f32[4096,256]{1,0:T(8,128)}, f32[256,4096]{1,0:T(8,128)}, f32[4096,256]{1,0:T(8,128)}, f32[1,256]{1,0:T(1,128)}, f32[75,256]{1,0:T(8,128)}, /*index...) custom-call(bf16[4096,256]{1,0:T(8,128)(2,1)} %get-tuple-element.25.sum_out, ...), custom_call_target="tpu_custom_call" | custom-call | tf_op jit(solution)/shard_map/finish/pallas_call | solution.py:1127

commit v4 on v3

--- a/solution.py
+++ b/solution.py
@@ -13,8 +13,8 @@
 POPART_PRIOR = 64.0
 NORM_EPS = 1e-06
 LOSS_WEIGHT = 256**-0.5
-SENDS = 148
-RECEIVES = 208
+SENDS = 156
+RECEIVES = 216
 
 
 MESH = pl.DeviceIdType.MESH
@@ -231,7 +231,7 @@
             peer,
         )
 
-    def open(self, produce):
+    def open(self, produce, between=None):
         self.seen = set()
         p = self.place
         for half in HALVES:
@@ -243,6 +243,8 @@
                     self.first + 14 + self.ORDER.index(where) * 2 + half,
                     p.partner,
                 )
+            if half == 1 and between is not None:
+                between()
             self.forward((2, 1), half, (), p.across, self.G)
             self.forward((1, 1), half, (), p.up, self.D)
             self.forward((3, 1), half, (), p.down, self.E)
@@ -429,39 +431,41 @@
 class RingGather:
     FROM_DOWN, FROM_UP, FAR = range(3)
 
-    def __init__(self, place, wires, view):
+    def __init__(self, place, wires, view, pieces):
         self.place = place
         self.wires = wires
         self.view = view
-        self.first = wires.claim(6)
-
-    def block(self, kind, half):
+        self.pieces = pieces
+        self.first = wires.claim(3 * pieces)
+
+    def block(self, kind, piece):
         dy = {self.FROM_DOWN: 3, self.FROM_UP: 1, self.FAR: 2}[kind]
-        return self.view(plus(self.place.y, dy, 4), half)
-
-    def post(self, v, kind, half, peer):
-        self.wires.send(v, v, self.first + kind * 2 + half, peer, "task")
-
-    def wait(self, kind, half):
-        self.wires.arrived(self.block(kind, half), self.first + kind * 2 + half, "task")
-
-    def open(self):
+        return self.view(plus(self.place.y, dy, 4), piece)
+
+    def post(self, v, kind, piece, peer):
+        self.wires.send(v, v, self.first + kind * self.pieces + piece, peer, "task")
+
+    def wait(self, kind, piece):
+        self.wires.arrived(
+            self.block(kind, piece), self.first + kind * self.pieces + piece, "task"
+        )
+
+    def open(self, piece):
         p = self.place
-        for up_half, down_half in ((0, 1), (1, 0)):
-            self.post(self.view(p.y, up_half), self.FROM_DOWN, up_half, p.up)
-            self.post(self.view(p.y, down_half), self.FROM_UP, down_half, p.down)
-
-    def relay(self):
-        self.wait(self.FROM_DOWN, 0)
-        self.post(self.block(self.FROM_DOWN, 0), self.FAR, 0, self.place.up)
-        self.wait(self.FROM_UP, 1)
-        self.post(self.block(self.FROM_UP, 1), self.FAR, 1, self.place.down)
+        v = self.view(p.y, piece)
+        self.post(v, self.FROM_DOWN, piece, p.up)
+        self.post(v, self.FROM_UP, piece, p.down)
+
+    def relay(self, piece):
+        kind = self.FROM_UP if piece % 2 else self.FROM_DOWN
+        self.wait(kind, piece)
+        peer = self.place.down if piece % 2 else self.place.up
+        self.post(self.block(kind, piece), self.FAR, piece, peer)
 
     def end(self):
-        self.wait(self.FROM_DOWN, 1)
-        self.wait(self.FROM_UP, 0)
-        self.wait(self.FAR, 0)
-        self.wait(self.FAR, 1)
+        for piece in range(self.pieces):
+            self.wait(self.FROM_DOWN if piece % 2 else self.FROM_UP, piece)
+            self.wait(self.FAR, piece)
 
 
 class RingExchange:
@@ -632,7 +636,7 @@
 
 
 def step_kernel(
-    own_tokens, gain, w_in, w_mix, w_out, head, vectors, tasks, actions, rewards, ends, behaviour,
+    own_tokens, gain, w_in, w_mix, w_out, head, head_bias, old_mean, old_scale, tasks, actions, rewards, ends, behaviour,
     sum_out_hbm, sum_mix_hbm, sum_in_hbm, new_head, stats,
     tokens, w_in_v, w_mix_v, w_out_v, pre_in, hidden_in, residual, gain_all, normed,
     pre_out, hidden_out, head_part, head_land, d_heads, stat_own, stat_land,
@@ -713,9 +717,10 @@
     scatter.open(lambda half: wide_product(hidden_in, w_mix_v, partial, half, False))
 
     for_hidden = RingGather(
-        task, wires, lambda y, half: hidden_ring.at[pl.ds(half * 8, 8), y]
-    )
-    for_hidden.open()
+        task, wires, lambda y, half: hidden_ring.at[pl.ds(half * 8, 8), y], 2
+    )
+    for_hidden.open(0)
+    for_hidden.open(1)
     core_rows = pl.ds(pl.multiple_of(place.c * 256, 256), 256)
     twin_rows = pl.ds(pl.multiple_of(256 - place.c * 256, 256), 256)
     for_tokens = RingExchange(
@@ -733,7 +738,15 @@
         statistics.wait(hop)
         summed = summed + stat_land[hop - 1]
     counts, totals, squares = summed[0:1, :], summed[1:2, :], summed[2:3, :]
-    bias, pop_mean, pop_scale = vectors[0:1, :], vectors[1:2, :], vectors[2:3, :]
+    small_rows = (head_bias, old_mean, old_scale)
+    bias, pop_mean, pop_scale = (
+        jnp.concatenate(
+            [ref[...], jnp.full((1, 128 - ref.shape[1]), fill, F32)], axis=1
+        )
+        for ref, fill in zip(small_rows, (0.0, 0.0, 1.0))
+    )
+    pop_mean, pop_scale = pltpu.roll(pop_mean, ACTIONS, 1), pltpu.roll(pop_scale, ACTIONS, 1)
+    pop_scale = jnp.where(lanes((1, 128)) < ACTIONS, 1.0, pop_scale)
     mean, scale = popart_update(counts, totals, squares, pop_mean, pop_scale)
     is_value = lanes((1, 128)) >= ACTIONS
     ratio = jnp.where(is_value, pop_scale / scale, 1.0)
@@ -772,7 +785,8 @@
         ).astype(BF16)
     spread = Gather(place, wires, row_view(normed), gather_b)
     spread.open()
-    for_hidden.relay()
+    for_hidden.relay(0)
+    for_hidden.relay(1)
     heads = AllPairs(wires, "tp", 16, head_land)
 
     def out_slab(dz):
@@ -831,8 +845,6 @@
         return carry
 
     lax.fori_loop(0, 4, pre_gradient, 0)
-    scatter = Scatter(place, wires, partial, twin_part_b, landing_b, scatter_slots)
-    scatter.open(lambda half: wide_product(d_pre_out, w_out_v, partial, half, True))
     for_out = TaskSum(task, wires, slab_rows(512), whole_out, land_out, x_out, sum_out)
     for_mix = TaskSum(task, wires, slab_cols, whole_mix, None, x_mix, sum_mix)
     for_in = TaskSum(task, wires, slab_rows(528), whole_in, None, x_in, sum_in)
@@ -878,12 +890,16 @@
     def out_product(dy):
         tall_product(normed, d_pre_out, whole_out, 512, dy)
 
-    out_product(2)
-    for_out.far()
-    scatter.finish_far()
+    def out_first():
+        out_product(2)
+        for_out.far()
+
+    scatter = Scatter(place, wires, partial, twin_part_b, landing_b, scatter_slots)
+    scatter.open(lambda half: wide_product(d_pre_out, w_out_v, partial, half, True), out_first)
     out_product(1)
     out_product(3)
     for_out.near()
+    scatter.finish_far()
     scatter.finish_across()
     out_product(0)
     for_out.relay()
@@ -938,12 +954,21 @@
         d = dot(arrived[rows, :], w_mix_v[...], ((1,), (1,)))
         d_pre_in[task.y, rows, :] = (d * slope(pre_in[rows, :])).astype(BF16)
 
-    gather.middle_near()
+    slabs = (0, 1, 3, 2)
+    for_slope = RingGather(
+        task,
+        wires,
+        lambda y, piece: d_pre_in.at[
+            y, pl.ds(pl.multiple_of(plus(place.z, slabs[piece], 4) * 128, 128), 128), :
+        ],
+        4,
+    )
     for_out.fold()
-    gather.middle_across()
-    gather.middle_far()
+    gather.middle()
+    for_out.finish()
     gather.wait_twin(gather.OWN, gather.ACROSS)
     hidden_slab(0)
+    for_slope.open(0)
     gather.late()
     for dy in (1, 3, 2):
         for_residual.wait(dy)
@@ -956,20 +981,17 @@
         gather_b,
     )
     ring.open()
-    for_out.finish()
     gather.wait_twin(gather.FROM_UP, gather.UP_ACROSS)
     hidden_slab(1)
+    for_slope.open(1)
     gather.last()
     gather.wait_twin(gather.FROM_DOWN, gather.DOWN_ACROSS)
     hidden_slab(3)
+    for_slope.open(2)
+    for_slope.relay(0)
     gather.wait_twin(gather.FAR, gather.FAR_ACROSS)
     hidden_slab(2)
-    for_slope = RingGather(
-        task,
-        wires,
-        lambda y, half: d_pre_in.at[y, pl.ds(half * 256, 256), :],
-    )
-    for_slope.open()
+    for_slope.open(3)
     small = dot(d_heads[...], hidden_out[...], ((0,), (0,)))
     bias = jnp.sum(d_heads[...].astype(F32), axis=0, keepdims=True)
     gain_total = jnp.sum(gain_parts[me], axis=0, keepdims=True)
@@ -984,12 +1006,12 @@
     small_rows = lambda y: small_own.at[pl.ds(pl.multiple_of(y * 32, 32), 32), :]
     for_small = RingExchange(task, wires, small_rows, lambda dy: small_land.at[dy - 1])
     for_small.open()
+    for_slope.relay(1)
+    for_slope.relay(2)
     ring.middle_near()
+    for_slope.relay(3)
     for_out.spread()
     ring.middle_across()
-    for_slope.relay()
-    ring.middle_far()
-    ring.late()
     for dy in (1, 2, 3):
         wires.arrived(far_tokens.at[dy - 1, twin_rows, :], token_slot + dy - 1)
     extra = small_rows(task.y)[...].astype(F32)
@@ -1001,20 +1023,22 @@
     for_slope.end()
     in_product(1 - task.xh)
     for_in.fold()
+    ring.middle_far()
+    in_product(task.xh)
+    ring.late()
     ring.last()
-    in_product(task.xh)
     ring.wait_twin(*range(8))
     mix_product(1 - task.xh)
     for_mix.fold()
     mix_product(task.xh)
+    for_in.finish()
     for_out.spread_far()
-    for_in.finish()
+    for_mix.finish()
     for_in.spread()
-    for_mix.finish()
-    for_in.spread_far()
     for_out.end()
     keep_out = load(sum_out, sum_out_hbm, local_sems, 4)
     for_mix.spread()
+    for_in.spread_far()
     for_in.end()
     keep_in = load(sum_in, sum_in_hbm, local_sems, 6)
     for_mix.spread_far()
@@ -1111,7 +1135,7 @@
             jax.ShapeDtypeStruct((128, 256), BF16),
             jax.ShapeDtypeStruct((8, 128), F32),
         ],
-        in_specs=[h, v, h, h, h, v, v, v, v, v, v, v],
+        in_specs=[h, v, h, h, h, v, v, v, v, v, v, v, v, v],
         out_specs=[h, h, h, v, v],
         scratch_shapes=[pltpu.VMEM(*s) for s in scratch]
         + [pltpu.SemaphoreType.DMA((SENDS,)), pltpu.SemaphoreType.DMA((RECEIVES,)), pltpu.SemaphoreType.DMA((7,))],
@@ -1159,14 +1183,6 @@
     observations, gain, w_in, w_mix, w_out, w_head, head_bias, pop_mean, pop_scale,
     task_indices, actions, rewards, episode_ends, behaviour_log_prob,
 ):
-    pad = (ACTIONS, 128 - ACTIONS - TASKS)
-    vectors = jnp.stack(
-        [
-            jnp.pad(head_bias, (0, 128 - ACTIONS - TASKS)),
-            jnp.pad(pop_mean, pad),
-            jnp.pad(pop_scale, pad, constant_values=1.0),
-        ]
-    )
     sums = step_call(
         observations.reshape(512, 256),
         gain.reshape(1, 256),
@@ -1174,7 +1190,9 @@
         w_mix,
         w_out,
         w_head.T,
-        vectors,
+        head_bias.reshape(1, ACTIONS + TASKS),
+        pop_mean.reshape(1, TASKS),
+        pop_scale.reshape(1, TASKS),
         task_indices.reshape(1, 32),
         actions.T,
         rewards.T,

time: 218 us -> 212 us (0.972); the launches traced: 215 us -> 212 us
  no operation moved by 1% of the time
where the time goes in v4:
time: 212 us
  Pallas kernels  211 us (100%)
    pallas_call x1, Pallas kernels, step_call(): pl.pallas_call(step_kernel, out_shape=[jax.ShapeDtypeStruct((4096, 256),...  203 us
    pallas_call x1, Pallas kernels, finish_call(): pl.pallas_call(finish_kernel, out_shape=[jax.ShapeDtypeStruct((4096, 256)...  7.93 us

profile of v4, /device:TPU:1, one launch (start us, length us, event | category | flops | bytes accessed | tf_op | source)
XLA Modules:
  0.0 211.6 jit_solution(10613262219799806848)
XLA Ops:
  0.6 202.9 %step.1 = (bf16[4096,256]{1,0:T(8,128)(2,1)}, bf16[256,4096]{1,0:T(8,128)(2,1)}, bf16[4224,256]{1,0:T(8,128)(2,1)}, bf16[128,256]{1,0:T(8,128)(2,1)}, f32[8,128]{1,0:T(8,128)}) custom-call(bf16[512,256]{1,0:T(8,128)(2,1)} %bitcast.18, f32[1,256]{1,0:T(1,128)} %bitcast.24, bf16[4096,256]{1,0:T(8,128)(2,1)} %w_in.1, bf16[256,4096]{1,0:T(8,128)(2,1)} %w_mix.1, ...), custom_call_target="tpu_custom_call" | custom-call | tf_op jit(solution)/shard_map/step/pallas_call | solution.py:1129
  203.6 7.9 %finish.1 = (f32[4096,256]{1,0:T(8,128)}, f32[256,4096]{1,0:T(8,128)}, f32[4096,256]{1,0:T(8,128)}, f32[1,256]{1,0:T(1,128)}, f32[75,256]{1,0:T(8,128)}, /*index...) custom-call(bf16[4096,256]{1,0:T(8,128)(2,1)} %get-tuple-element.25.sum_out, ...), custom_call_target="tpu_custom_call" | custom-call | tf_op jit(solution)/shard_map/finish/pallas_call | solution.py:1151

commit v5 on v4

--- a/solution.py
+++ b/solution.py
@@ -13,8 +13,8 @@
 POPART_PRIOR = 64.0
 NORM_EPS = 1e-06
 LOSS_WEIGHT = 256**-0.5
-SENDS = 156
-RECEIVES = 216
+SENDS = 172
+RECEIVES = 244
 
 
 MESH = pl.DeviceIdType.MESH
@@ -85,11 +85,12 @@
 class Gather:
     ACROSS, FROM_DOWN, FROM_UP, DOWN_ACROSS, UP_ACROSS, FAR, FAR_ACROSS, OWN = range(8)
 
-    def __init__(self, place, wires, view, first):
+    def __init__(self, place, wires, view, first, far_across_on_z=False):
         self.place = place
         self.wires = wires
         self.view = view
         self.first = first
+        self.on_z = far_across_on_z
         p = place
         self.block = {
             self.ACROSS: p.at(0, 1),
@@ -167,13 +168,17 @@
     def middle_far(self):
         for half in HALVES:
             self.wait(self.FAR, half)
-            self.pass_on(self.FAR, half, self.place.across, self.FAR_ACROSS)
+            if not self.on_z:
+                self.pass_on(self.FAR, half, self.place.across, self.FAR_ACROSS)
             self.to_twin(self.FAR, half)
 
     def late(self):
         for half in HALVES:
             for kind in (self.DOWN_ACROSS, self.UP_ACROSS):
                 self.wait(kind, half)
+                if self.on_z and (kind == self.UP_ACROSS) == (half == 1):
+                    peer = self.place.down if half else self.place.up
+                    self.pass_on(kind, half, peer, self.FAR_ACROSS)
                 self.to_twin(kind, half)
 
     def last(self):
@@ -497,8 +502,13 @@
     return lambda ref, n: ref.at[pl.ds(pl.multiple_of(n * height, 16), height), :]
 
 
-def slab_cols(ref, n):
-    return ref.at[:, pl.ds(pl.multiple_of(n * 512, 512), 512)]
+def tall_piece(piece):
+    size = 272 if piece else 256
+    return lambda ref, n: ref.at[pl.ds(pl.multiple_of(n * 528 + piece * 256, 16), size), :]
+
+
+def wide_piece(piece):
+    return lambda ref, n: ref.at[:, pl.ds(pl.multiple_of(n * 512 + piece * 256, 256), 256)]
 
 
 def popart_update(counts, totals, squares, pop_mean, pop_scale):
@@ -846,8 +856,13 @@
 
     lax.fori_loop(0, 4, pre_gradient, 0)
     for_out = TaskSum(task, wires, slab_rows(512), whole_out, land_out, x_out, sum_out)
-    for_mix = TaskSum(task, wires, slab_cols, whole_mix, None, x_mix, sum_mix)
-    for_in = TaskSum(task, wires, slab_rows(528), whole_in, None, x_in, sum_in)
+    mixes = [
+        TaskSum(task, wires, wide_piece(n), whole_mix, None, x_mix.at[n], sum_mix) for n in (0, 1)
+    ]
+    x_pieces = (x_in.at[pl.ds(0, 256), :], x_in.at[pl.ds(256, 272), :])
+    ins = [
+        TaskSum(task, wires, tall_piece(n), whole_in, None, x_pieces[n], sum_in) for n in (0, 1)
+    ]
 
     def tall_product(left, right, whole, height, dy):
         k = plus(task.y, dy, 4)
@@ -861,31 +876,23 @@
 
         lax.fori_loop(0, 4, tile, 0)
 
-    def mix_product(part):
-        def tile(n, carry):
-            at = pl.multiple_of(part * 512 + n * 256, 256)
-            whole_mix[:, pl.ds(at, 256)] = dot(
-                hidden_t[...], residual_ring[:, pl.ds(at, 256)]
-            ).astype(BF16)
-            return carry
-
-        lax.fori_loop(0, 2, tile, 0)
-
-    def in_product(part):
-        def tile(n, carry):
-            at = pl.multiple_of(part * 512 + n * 256, 256)
-            here = pl.ds(pl.multiple_of(task.y * 1024 + at, 256), 256)
-            value = dot(tokens[pl.ds(0, 512), here], d_pre_in[task.y], ((0,), (0,)))
-            for dy in (1, 2, 3):
-                value = value + dot(
-                    far_tokens[dy - 1, :, pl.ds(at, 256)],
-                    d_pre_in[plus(task.y, dy, 4)],
-                    ((0,), (0,)),
-                )
-            whole_in[pl.ds(pl.multiple_of(part * 528 + n * 256, 16), 256), :] = value.astype(BF16)
-            return carry
-
-        lax.fori_loop(0, 2, tile, 0)
+    def mix_product(part, n):
+        at = pl.multiple_of(part * 512 + n * 256, 256)
+        whole_mix[:, pl.ds(at, 256)] = dot(
+            hidden_t[...], residual_ring[:, pl.ds(at, 256)]
+        ).astype(BF16)
+
+    def in_product(part, n):
+        at = pl.multiple_of(part * 512 + n * 256, 256)
+        here = pl.ds(pl.multiple_of(task.y * 1024 + at, 256), 256)
+        value = dot(tokens[pl.ds(0, 512), here], d_pre_in[task.y], ((0,), (0,)))
+        for dy in (1, 2, 3):
+            value = value + dot(
+                far_tokens[dy - 1, :, pl.ds(at, 256)],
+                d_pre_in[plus(task.y, dy, 4)],
+                ((0,), (0,)),
+            )
+        whole_in[pl.ds(pl.multiple_of(part * 528 + n * 256, 16), 256), :] = value.astype(BF16)
 
     def out_product(dy):
         tall_product(normed, d_pre_out, whole_out, 512, dy)
@@ -979,6 +986,7 @@
             pl.ds(pl.multiple_of(block * 128, 128), 128), pl.ds(half * 512, 512)
         ],
         gather_b,
+        True,
     )
     ring.open()
     gather.wait_twin(gather.FROM_UP, gather.UP_ACROSS)
@@ -1021,28 +1029,42 @@
     for part in (0, 1):
         whole_in[pl.ds(part * 528 + 512, 16), :] = extra[part * 16 : part * 16 + 16, :].astype(BF16)
     for_slope.end()
-    in_product(1 - task.xh)
-    for_in.fold()
+    in_product(1 - task.xh, 0)
+    ins[0].fold()
+    in_product(1 - task.xh, 1)
+    ins[1].fold()
     ring.middle_far()
-    in_product(task.xh)
+    in_product(task.xh, 0)
     ring.late()
+    in_product(task.xh, 1)
+    ins[0].finish()
     ring.last()
+    ins[1].finish()
     ring.wait_twin(*range(8))
-    mix_product(1 - task.xh)
-    for_mix.fold()
-    mix_product(task.xh)
-    for_in.finish()
+    mix_product(1 - task.xh, 0)
+    mixes[0].fold()
+    mix_product(1 - task.xh, 1)
+    mixes[1].fold()
+    mix_product(task.xh, 0)
+    mix_product(task.xh, 1)
     for_out.spread_far()
-    for_mix.finish()
-    for_in.spread()
+    ins[0].spread()
+    ins[1].spread()
+    mixes[0].finish()
+    ins[0].spread_far()
+    mixes[1].finish()
+    ins[1].spread_far()
+    mixes[0].spread()
+    mixes[1].spread()
     for_out.end()
     keep_out = load(sum_out, sum_out_hbm, local_sems, 4)
-    for_mix.spread()
-    for_in.spread_far()
-    for_in.end()
+    mixes[0].spread_far()
+    mixes[1].spread_far()
+    ins[0].end()
+    ins[1].end()
     keep_in = load(sum_in, sum_in_hbm, local_sems, 6)
-    for_mix.spread_far()
-    for_mix.end()
+    mixes[0].end()
+    mixes[1].end()
     keep_mix = load(sum_mix, sum_mix_hbm, local_sems, 5)
     wires.drain()
     for keep in (keep_out, keep_mix, keep_in):
@@ -1123,7 +1145,7 @@
         ((16, 8, 256), F32), ((15, 8, 256), F32),
         ((4096, 256), BF16), ((256, 1024), BF16), ((1056, 256), BF16),
         ((3, 2, 512, 256), BF16),
-        ((512, 256), BF16), ((256, 512), BF16), ((528, 256), BF16),
+        ((512, 256), BF16), ((2, 256, 256), BF16), ((528, 256), BF16),
         ((4096, 256), BF16), ((256, 4096), BF16), ((4224, 256), BF16),
     ]
     return pl.pallas_call(

time: 212 us -> 200 us (0.943)
  Pallas kernels: 211 us -> 199 us
    pallas_call x1, Pallas kernels: 203 us -> 191 us  [step_call(): pl.pallas_call(step_kernel, out_shape=[jax.ShapeDtypeStruct((4096, 256),...]
where the time goes in v5:
time: 200 us
  Pallas kernels  199 us (100%)
    pallas_call x1, Pallas kernels, step_call(): pl.pallas_call(step_kernel, out_shape=[jax.ShapeDtypeStruct((4096, 256),...  191 us
    pallas_call x1, Pallas kernels, finish_call(): pl.pallas_call(finish_kernel, out_shape=[jax.ShapeDtypeStruct((4096, 256)...  7.93 us

profile of v5, /device:TPU:1, one launch (start us, length us, event | category | flops | bytes accessed | tf_op | source)
XLA Modules:
  0.0 200.1 jit_solution(15307369853645705832)
XLA Ops:
  0.6 191.3 %step.1 = (bf16[4096,256]{1,0:T(8,128)(2,1)}, bf16[256,4096]{1,0:T(8,128)(2,1)}, bf16[4224,256]{1,0:T(8,128)(2,1)}, bf16[128,256]{1,0:T(8,128)(2,1)}, f32[8,128]{1,0:T(8,128)}) custom-call(bf16[512,256]{1,0:T(8,128)(2,1)} %bitcast.18, f32[1,256]{1,0:T(1,128)} %bitcast.24, bf16[4096,256]{1,0:T(8,128)(2,1)} %w_in.1, bf16[256,4096]{1,0:T(8,128)(2,1)} %w_mix.1, ...), custom_call_target="tpu_custom_call" | custom-call | tf_op jit(solution)/shard_map/step/pallas_call | solution.py:1151
  192.0 7.9 %finish.1 = (f32[4096,256]{1,0:T(8,128)}, f32[256,4096]{1,0:T(8,128)}, f32[4096,256]{1,0:T(8,128)}, f32[1,256]{1,0:T(1,128)}, f32[75,256]{1,0:T(8,128)}, /*index...) custom-call(bf16[4096,256]{1,0:T(8,128)(2,1)} %get-tuple-element.25.sum_out, ...), custom_call_target="tpu_custom_call" | custom-call | tf_op jit(solution)/shard_map/finish/pallas_call | solution.py:1173

commit v6 on v5

--- a/solution.py
+++ b/solution.py
@@ -13,8 +13,8 @@
 POPART_PRIOR = 64.0
 NORM_EPS = 1e-06
 LOSS_WEIGHT = 256**-0.5
-SENDS = 172
-RECEIVES = 244
+SENDS = 176
+RECEIVES = 218
 
 
 MESH = pl.DeviceIdType.MESH
@@ -330,7 +330,7 @@
         self.land = land
         self.land_x = land_x
         self.result = result
-        self.first = wires.claim(14)
+        self.first = wires.claim(8) - 6 if land is None else wires.claim(14)
 
     def slab(self, ref, dy, part):
         return self.view(ref, plus(self.place.y, dy, 4) * 2 + part)
@@ -431,6 +431,66 @@
     def end(self):
         self.get(self.FAR)
         self.get(self.FAR_ACROSS)
+
+
+class RingFirst:
+    FROM_DOWN, FROM_UP, FAR, OWN = range(4)
+
+    def __init__(self, sums):
+        self.sums = sums
+        self.place = sums.place
+        self.first = sums.wires.claim(14)
+
+    def halves(self, dy, across, half):
+        xh = self.place.xh
+        slab = self.sums.slab(self.sums.result, dy, 1 - xh if across else xh)
+        return slab.at[:, pl.ds(half * 128, 128)]
+
+    def held(self, kind, half):
+        return self.halves({self.FROM_DOWN: 3, self.FROM_UP: 1, self.FAR: 2}[kind], 0, half)
+
+    def along(self, v, kind, half, peer):
+        self.sums.wires.send(v, v, self.first + kind * 2 + half, peer, "task")
+
+    def over(self, dy):
+        whole = self.sums.slab(self.sums.result, dy, self.place.xh)
+        self.sums.wires.send(whole, whole, self.first + 6 + dy, self.place.across, "task")
+
+    def wait(self, kind, half):
+        self.sums.wires.arrived(self.held(kind, half), self.first + kind * 2 + half, "task")
+
+    def finish(self):
+        p, sums = self.place, self.sums
+        sums.wait(sums.land_x, 6)
+        own = sums.held(sums.OWN)
+        own[...] = (sums.local(p.xh) + sums.land_x[...].astype(F32)).astype(BF16)
+        for up_half, down_half in ((0, 1), (1, 0)):
+            self.along(self.halves(0, 0, up_half), self.FROM_DOWN, up_half, p.up)
+            self.along(self.halves(0, 0, down_half), self.FROM_UP, down_half, p.down)
+        self.over(0)
+
+    def relay(self):
+        for kind, half, peer in (
+            (self.FROM_DOWN, 0, self.place.up), (self.FROM_UP, 1, self.place.down)
+        ):
+            self.wait(kind, half)
+            self.along(self.held(kind, half), self.FAR, half, peer)
+
+    def cross(self):
+        self.wait(self.FROM_DOWN, 1)
+        self.over(3)
+        self.wait(self.FROM_UP, 0)
+        self.over(1)
+
+    def cross_far(self):
+        self.wait(self.FAR, 0)
+        self.wait(self.FAR, 1)
+        self.over(2)
+
+    def end(self):
+        for dy in range(4):
+            whole = self.sums.slab(self.sums.result, dy, 1 - self.place.xh)
+            self.sums.wires.arrived(whole, self.first + 6 + dy, "task")
 
 
 class RingGather:
@@ -527,13 +587,13 @@
 
 
 class AllPairs:
-    def __init__(self, wires, axis, size, land):
+    def __init__(self, wires, axis, size, land, first=None):
         self.wires = wires
         self.axis = axis
         self.size = size
         self.here = lax.axis_index(axis)
         self.land = land
-        self.first = wires.claim(size - 1)
+        self.first = wires.claim(size - 1) if first is None else first
 
     def post(self, peer_at, src):
         peer = plus(self.here, peer_at, self.size)
@@ -859,6 +919,7 @@
     mixes = [
         TaskSum(task, wires, wide_piece(n), whole_mix, None, x_mix.at[n], sum_mix) for n in (0, 1)
     ]
+    last_mix = RingFirst(mixes[1])
     x_pieces = (x_in.at[pl.ds(0, 256), :], x_in.at[pl.ds(256, 272), :])
     ins = [
         TaskSum(task, wires, tall_piece(n), whole_in, None, x_pieces[n], sum_in) for n in (0, 1)
@@ -952,7 +1013,7 @@
         gain_rows = gain_rows + d_normed[pl.ds(m * 8, 8), :]
     for n in range(16):
         gain_parts[n] = gain_rows[:, n * 256 : n * 256 + 256]
-    gains = AllPairs(wires, "tp", 16, gain_land)
+    gains = AllPairs(wires, "tp", 16, gain_land, heads.first)
     for hop in range(1, 16):
         gains.post(hop, lambda peer: gain_parts.at[peer])
 
@@ -1016,8 +1077,8 @@
     for_small.open()
     for_slope.relay(1)
     for_slope.relay(2)
+    for_slope.relay(3)
     ring.middle_near()
-    for_slope.relay(3)
     for_out.spread()
     ring.middle_across()
     for dy in (1, 2, 3):
@@ -1052,19 +1113,20 @@
     ins[1].spread()
     mixes[0].finish()
     ins[0].spread_far()
-    mixes[1].finish()
+    last_mix.finish()
     ins[1].spread_far()
     mixes[0].spread()
-    mixes[1].spread()
+    last_mix.relay()
+    last_mix.cross()
     for_out.end()
     keep_out = load(sum_out, sum_out_hbm, local_sems, 4)
     mixes[0].spread_far()
-    mixes[1].spread_far()
+    last_mix.cross_far()
     ins[0].end()
     ins[1].end()
     keep_in = load(sum_in, sum_in_hbm, local_sems, 6)
     mixes[0].end()
-    mixes[1].end()
+    last_mix.end()
     keep_mix = load(sum_mix, sum_mix_hbm, local_sems, 5)
     wires.drain()
     for keep in (keep_out, keep_mix, keep_in):

time: 200 us -> 200 us (level)
  no operation moved by 1% of the time
where the time goes in v6:
time: 200 us; the launch traced here: 199 us
  Pallas kernels  199 us (100%)
    pallas_call x1, Pallas kernels, step_call(): pl.pallas_call(step_kernel, out_shape=[jax.ShapeDtypeStruct((4096, 256),...  191 us
    pallas_call x1, Pallas kernels, finish_call(): pl.pallas_call(finish_kernel, out_shape=[jax.ShapeDtypeStruct((4096, 256)...  7.93 us

profile of v6, /device:TPU:1, one launch (start us, length us, event | category | flops | bytes accessed | tf_op | source)
XLA Modules:
  0.0 199.4 jit_solution(1490135582496423398)
XLA Ops:
  0.6 190.6 %step.1 = (bf16[4096,256]{1,0:T(8,128)(2,1)}, bf16[256,4096]{1,0:T(8,128)(2,1)}, bf16[4224,256]{1,0:T(8,128)(2,1)}, bf16[128,256]{1,0:T(8,128)(2,1)}, f32[8,128]{1,0:T(8,128)}) custom-call(bf16[512,256]{1,0:T(8,128)(2,1)} %bitcast.18, f32[1,256]{1,0:T(1,128)} %bitcast.24, bf16[4096,256]{1,0:T(8,128)(2,1)} %w_in.1, bf16[256,4096]{1,0:T(8,128)(2,1)} %w_mix.1, ...), custom_call_target="tpu_custom_call" | custom-call | tf_op jit(solution)/shard_map/step/pallas_call | solution.py:1213
  191.3 7.9 %finish.1 = (f32[4096,256]{1,0:T(8,128)}, f32[256,4096]{1,0:T(8,128)}, f32[4096,256]{1,0:T(8,128)}, f32[1,256]{1,0:T(1,128)}, f32[75,256]{1,0:T(8,128)}, /*index...) custom-call(bf16[4096,256]{1,0:T(8,128)(2,1)} %get-tuple-element.25.sum_out, ...), custom_call_target="tpu_custom_call" | custom-call | tf_op jit(solution)/shard_map/finish/pallas_call | solution.py:1235

commit v7 on v6

--- a/solution.py
+++ b/solution.py
@@ -13,8 +13,8 @@
 POPART_PRIOR = 64.0
 NORM_EPS = 1e-06
 LOSS_WEIGHT = 256**-0.5
-SENDS = 176
-RECEIVES = 218
+SENDS = 144
+RECEIVES = 217
 
 
 MESH = pl.DeviceIdType.MESH
@@ -47,6 +47,7 @@
         self.send_sems = send_sems
         self.recv_sems = recv_sems
         self.sent = []
+        self.free = list(range(SENDS))
         self.slots = 0
 
     def claim(self, count):
@@ -55,16 +56,17 @@
         return first
 
     def send(self, src, dst, slot, peer, axis="tp"):
+        at = self.free.pop(0)
         copy = pltpu.make_async_remote_copy(
             src_ref=src,
             dst_ref=dst,
-            send_sem=self.send_sems.at[len(self.sent)],
+            send_sem=self.send_sems.at[at],
             recv_sem=self.recv_sems.at[slot],
             device_id={axis: peer},
             device_id_type=MESH,
         )
         copy.start()
-        self.sent.append(copy)
+        self.sent.append((copy, at, axis))
 
     def arrived(self, dst, slot, axis="tp"):
         pltpu.make_async_remote_copy(
@@ -76,10 +78,15 @@
             device_id_type=MESH,
         ).wait_recv()
 
-    def drain(self):
-        for copy in self.sent:
-            copy.wait_send()
-        self.sent = []
+    def drain(self, axes=("tp", "task")):
+        kept = []
+        for copy, at, axis in self.sent:
+            if axis in axes:
+                copy.wait_send()
+                self.free.append(at)
+            else:
+                kept.append((copy, at, axis))
+        self.sent = kept
 
 
 class Gather:
@@ -783,6 +790,7 @@
 
     lax.fori_loop(0, 4, activate, 0)
     get_mix.wait()
+    wires.drain(("tp",))
     scatter = Scatter(place, wires, partial, twin_part, landing, scatter_slots)
     scatter.open(lambda half: wide_product(hidden_in, w_mix_v, partial, half, False))
 
@@ -988,6 +996,7 @@
         step = inverse * scaled - v * (inverse * inverse * inverse * inner * (1.0 / 4096))
         arrived[pl.ds(pl.multiple_of(me * 32 + m * 16, 16), 16), :] = step.astype(BF16)
         d_normed[r, :] = d * v * inverse
+    wires.drain(("tp",))
     gather = Gather(place, wires, row_view(arrived), gather_a)
     gather.open()
     ring_rows = lambda y: pl.ds(pl.multiple_of(me * 128 + y * 32, 32), 32)

time: 200 us -> 199 us (level)
  no operation moved by 1% of the time
where the time goes in v7:
time: 199 us
  Pallas kernels  198 us (99%)
    pallas_call x1, Pallas kernels, step_call(): pl.pallas_call(step_kernel, out_shape=[jax.ShapeDtypeStruct((4096, 256),...  190 us
    pallas_call x1, Pallas kernels, finish_call(): pl.pallas_call(finish_kernel, out_shape=[jax.ShapeDtypeStruct((4096, 256)...  7.93 us

profile of v7, /device:TPU:1, one launch (start us, length us, event | category | flops | bytes accessed | tf_op | source)
XLA Modules:
  0.0 199.1 jit_solution(16792301667700039984)
XLA Ops:
  0.6 190.4 %step.1 = (bf16[4096,256]{1,0:T(8,128)(2,1)}, bf16[256,4096]{1,0:T(8,128)(2,1)}, bf16[4224,256]{1,0:T(8,128)(2,1)}, bf16[128,256]{1,0:T(8,128)(2,1)}, f32[8,128]{1,0:T(8,128)}) custom-call(bf16[512,256]{1,0:T(8,128)(2,1)} %bitcast.18, f32[1,256]{1,0:T(1,128)} %bitcast.24, bf16[4096,256]{1,0:T(8,128)(2,1)} %w_in.1, bf16[256,4096]{1,0:T(8,128)(2,1)} %w_mix.1, ...), custom_call_target="tpu_custom_call" | custom-call | tf_op jit(solution)/shard_map/step/pallas_call | solution.py:1222
  191.1 7.9 %finish.1 = (f32[4096,256]{1,0:T(8,128)}, f32[256,4096]{1,0:T(8,128)}, f32[4096,256]{1,0:T(8,128)}, f32[1,256]{1,0:T(1,128)}, f32[75,256]{1,0:T(8,128)}, /*index...) custom-call(bf16[4096,256]{1,0:T(8,128)(2,1)} %get-tuple-element.25.sum_out, ...), custom_call_target="tpu_custom_call" | custom-call | tf_op jit(solution)/shard_map/finish/pallas_call | solution.py:1244
